TPU v7x, 32 devices: a whole 2x2x4 slice. The times are simulated.
32 devices in a mesh: seq: 32 (over z, y, x, core).
Axes of the slice: x: 2, y: 2, z: 4, core: 2. Of those that a mesh axis runs over, the one named last changes fastest.
Arguments:
- residual: bfloat16 [4096, 2560], P('seq'), may hold values from -6 to 6
- queries: bfloat16 [4096, 2560], P('seq'), may hold values from -5 to 5, as said below
- keys: bfloat16 [4096, 512], P('seq'), may hold values from -5 to 5
- values: bfloat16 [4096, 512], P('seq'), may hold values from -6 to 6
- out_proj: bfloat16 [2560, 2560], P(None, 'seq'), may hold values from -0.125 to 0.125
- norm_gain: float32 [2560], replicated, may hold values from 0.25 to 1.75
- expert_in: bfloat16 [2560, 2, 106496], P(None, None, 'seq'), may hold values from -0.125 to 0.125
- expert_down: bfloat16 [106496, 2560], P('seq'), may hold values from -0.15625 to 0.15625
- routes: int32 [4096, 2], P('seq'), may hold values from 0 to 63, all different within a row
- gate_ints: int32 [4096, 2], P('seq'), may hold values from 1 to 1023
- modality: int32 [4096], P('seq'), may hold values 0 or 1
- capacity: int32 [64, 2], replicated, may hold values from 1 to 2, as said below
Outputs:
- attended: bfloat16 [4096, 2560], P('seq')
- expert_mix: bfloat16 [4096, 2560], P('seq')
Inputs may be any that keep to these rules, and one draw needn't show every extreme that they name: `queries` and `keys`: every element lies between -5 and 5. `routes`: each token names two different experts. `capacity`: some entry equals 2.
All inputs are finite; a program needn't handle non-finite values. No bound on the sum of `modality` on one device may be relied on, other than what follows from the above.
Results may differ from a plain program's by a relative error of at most 0.0086.
Values may be sent and summed in bfloat16 or wider, within the bound.
No kernel may reach another device: no remote copies, remote signals or barrier semaphores. Data moves between devices by JAX's collectives and lax.ppermute only.
A program may use at most 192 MiB of HBM per device.

v0:
```python
import jax
import jax.numpy as jnp
from jax import lax
from jax.sharding import PartitionSpec as P

HEADS = 20
KV_HEADS = 4
HEAD = 128
WINDOW = 1024
EXPERTS = 64
CAP = 2


def shifted(value, axis, steps):
    count = lax.axis_size(axis)
    initial, last = (max(0, -steps), min(count, count - steps))
    return lax.ppermute(value, axis, [(source, source + steps) for source in range(initial, last)])


def body(
    residual,
    queries,
    keys,
    values,
    out_proj,
    norm_gain,
    expert_in,
    expert_down,
    routes,
    gate_ints,
    modality,
    capacity,
):
    devices = lax.axis_size("seq")
    device_pos = lax.axis_index("seq")
    tok_rows = residual.shape[0]
    width_d = residual.shape[1]
    q_group = HEADS // KV_HEADS
    blocks_back = (WINDOW + tok_rows - 1) // tok_rows
    earlier = []
    moving = (keys, values)
    for step_back in range(blocks_back):
        moving = shifted((moving[0], moving[1]), "seq", 1)
        earlier.insert(0, moving)
    all_keys = jnp.concatenate([pair_kv[0] for pair_kv in earlier] + [keys], 0)
    all_values = jnp.concatenate([pair_kv[1] for pair_kv in earlier] + [values], 0)
    key_span = all_keys.shape[0]
    q_pos = device_pos * tok_rows + jnp.arange(tok_rows, dtype=jnp.int32)
    k_pos = (device_pos - blocks_back) * tok_rows + jnp.arange(key_span, dtype=jnp.int32)
    visible = (
        (k_pos[None, :] <= q_pos[:, None])
        & (k_pos[None, :] > q_pos[:, None] - WINDOW)
        & (k_pos[None, :] >= 0)
    )
    score_scale = HEAD ** (-0.5)
    query_heads = jnp.transpose(queries.reshape(tok_rows, KV_HEADS, q_group, HEAD), (1, 0, 2, 3))
    key_heads = jnp.transpose(all_keys.reshape(key_span, KV_HEADS, HEAD), (1, 0, 2))
    value_heads = jnp.transpose(all_values.reshape(key_span, KV_HEADS, HEAD), (1, 0, 2))

    def one_head(operands):
        q_one, k_one, v_one = operands
        scores = (
            jnp.einsum("qgd,kd->gqk", q_one, k_one, preferred_element_type=jnp.float32)
            * score_scale
        )
        scores = jnp.where(visible[None], scores, -jnp.inf)
        row_max = jnp.max(scores, -1, keepdims=True)
        weights_raw = jnp.exp(scores - row_max)
        probs_bf = (weights_raw / jnp.sum(weights_raw, -1, keepdims=True)).astype(jnp.bfloat16)
        return jnp.einsum(
            "gqk,kd->qgd", probs_bf, v_one, preferred_element_type=jnp.float32
        ).astype(jnp.bfloat16)

    context = lax.map(one_head, (query_heads, key_heads, value_heads))
    context = jnp.transpose(context, (1, 0, 2, 3)).reshape(tok_rows, HEADS * HEAD)
    attended = jnp.dot(
        context,
        lax.all_gather(out_proj, "seq", axis=1, tiled=True),
        preferred_element_type=jnp.float32,
    ).astype(jnp.bfloat16)
    attended = lax.optimization_barrier(attended)
    hidden = residual.astype(jnp.float32) + attended.astype(jnp.float32)
    normed = (
        hidden * lax.rsqrt(jnp.mean(hidden * hidden, -1, keepdims=True) + 1e-05) * norm_gain
    ).astype(jnp.bfloat16)
    slot_count = 2 * CAP
    split_ways = max(1, devices // EXPERTS)
    local_experts = max(1, EXPERTS // devices)
    chosen = routes.reshape(-1)
    modal_flag = jnp.repeat(modality, 2)
    slot_key = chosen * 2 + modal_flag
    onehot = (slot_key[:, None] == jnp.arange(2 * EXPERTS, dtype=jnp.int32)[None, :]).astype(
        jnp.int32
    )
    rank_in = jnp.sum((jnp.cumsum(onehot, 0) - onehot) * onehot, 1)
    limit_of = jnp.sum(onehot * capacity.reshape(1, -1), 1)
    kept_mask = rank_in < limit_of
    column = chosen * slot_count + modal_flag * CAP + rank_in
    select = (
        (column[:, None] == jnp.arange(EXPERTS * slot_count, dtype=jnp.int32)[None, :])
        & kept_mask[:, None]
    ).astype(jnp.bfloat16)
    doubled = jnp.repeat(normed, 2, axis=0)
    slot_table = lax.dot_general(
        select, doubled, (((0,), (0,)), ((), ())), preferred_element_type=jnp.float32
    ).astype(jnp.bfloat16)
    slab_cols = expert_in.shape[2]
    hidden_each = slab_cols // local_experts
    weights_in = expert_in.reshape(width_d, 2, local_experts, hidden_each)
    weights_down = expert_down.reshape(local_experts, hidden_each, width_d)
    outgoing = jnp.repeat(slot_table.reshape(EXPERTS, slot_count, width_d), split_ways, 0)
    outgoing = outgoing.reshape(devices, local_experts, slot_count, width_d)
    gate_up = jnp.einsum(
        "nlkd,dglf->glnkf",
        lax.all_to_all(outgoing, "seq", split_axis=0, concat_axis=0, tiled=True),
        weights_in,
        preferred_element_type=jnp.float32,
    )
    active = (jax.nn.silu(gate_up[0]) * gate_up[1]).astype(jnp.bfloat16)
    partial_value = jnp.einsum(
        "lnkf,lfd->nlkd", active, weights_down, preferred_element_type=jnp.float32
    )
    computed = lax.optimization_barrier(partial_value.astype(jnp.bfloat16))
    returned = lax.all_to_all(computed, "seq", split_axis=0, concat_axis=0, tiled=True)
    summed = jnp.sum(
        returned.reshape(EXPERTS, split_ways, slot_count, width_d).astype(jnp.float32), 1
    )
    mixed = summed.astype(jnp.bfloat16).reshape(EXPERTS * slot_count, width_d)
    gathered_rows = jnp.dot(select, mixed, preferred_element_type=jnp.float32).reshape(
        tok_rows, 2, width_d
    )
    gate_scale = jnp.where(
        kept_mask, gate_ints.reshape(-1).astype(jnp.float32) / 1024.0, 0.0
    ).reshape(tok_rows, 2, 1)
    expert_mix = jnp.sum(gate_scale * gathered_rows, 1).astype(jnp.bfloat16)
    return (attended, expert_mix)


def solution(mesh):
    placed = (
        P("seq", None),
        P("seq", None),
        P("seq", None),
        P("seq", None),
        P(None, "seq"),
        P(),
        P(None, None, "seq"),
        P("seq", None),
        P("seq", None),
        P("seq", None),
        P("seq"),
        P(),
    )
    return jax.shard_map(
        body,
        mesh=mesh,
        in_specs=placed,
        out_specs=(P("seq", None), P("seq", None)),
        check_vma=False,
    )
```

profile of v0, /device:TPU:0, one launch (start us, length us, event | category | flops | bytes accessed | tf_op | source)
XLA Modules:
  0.0 316.1 jit_solution(2247563732822306015)
XLA Ops:
  7.9 2.4 collective-permute-start
  11.4 4.5 %collective-permute-start.8 = (bf16[128,512]{0,1:T(8,128)(2,1)S(1)}, bf16[128,512]{0,1:T(8,128)(2,1)S(1)}, u32[]{:S(2)}, u32[]{:S(2)}) collective-permute-start(bf16[128,512]{0,1:T(8,128)(2,1)S(1)} %copy.92), channel_id=1, source_target_pairs={{0,1},{1,2},{2,3},{3,4},{4,5},{5,6},{6,7},{7,8},{8,9},{9,10},{10,1... | collective-permute-start | bytes 393224 | tf_op jit(solution)/shard_map/ppermute | solution.py:17
  19.9 3.5 %collective-permute-start.9 = (bf16[128,512]{0,1:T(8,128)(2,1)S(1)}, bf16[128,512]{0,1:T(8,128)(2,1)S(1)}, u32[]{:S(2)}, u32[]{:S(2)}) collective-permute-start(bf16[128,512]{0,1:T(8,128)(2,1)S(1)} %collective-permute-done.8), channel_id=1, source_target_pairs={{0,1},{1,2},{2,3},{3,4},{4,5},{5,6},{6,7},{7,8},{8,9},{9,10},{10,1... | collective-permute-start | bytes 393224 | tf_op jit(solution)/shard_map/ppermute | solution.py:17
  25.5 3.7 %collective-permute-start.10 = (bf16[128,512]{0,1:T(8,128)(2,1)S(1)}, bf16[128,512]{0,1:T(8,128)(2,1)S(1)}, u32[]{:S(2)}, u32[]{:S(2)}) collective-permute-start(bf16[128,512]{0,1:T(8,128)(2,1)S(1)} %collective-permute-done.9), channel_id=1, source_target_pairs={{0,1},{1,2},{2,3},{3,4},{4,5},{5,6},{6,7},{7,8},{8,9},{9,10},{10,1... | collective-permute-start | bytes 393224 | tf_op jit(solution)/shard_map/ppermute | solution.py:17
  29.2 4.3 %collective-permute-start.3 = (bf16[128,512]{1,0:T(8,128)(2,1)S(1)}, bf16[128,512]{1,0:T(8,128)(2,1)S(1)}, u32[]{:S(2)}, u32[]{:S(2)}) collective-permute-start(bf16[128,512]{1,0:T(8,128)(2,1)S(1)} %collective-permute-done.2), channel_id=1, source_target_pairs={{0,1},{1,2},{2,3},{3,4},{4,5},{5,6},{6,7},{7,8},{8,9},{9,10},{10,1... | collective-permute-start | bytes 393224 | tf_op jit(solution)/shard_map/ppermute | solution.py:17
  35.5 4.6 %collective-permute-start.4 = (bf16[128,512]{1,0:T(8,128)(2,1)S(1)}, bf16[128,512]{1,0:T(8,128)(2,1)S(1)}, u32[]{:S(2)}, u32[]{:S(2)}) collective-permute-start(bf16[128,512]{1,0:T(8,128)(2,1)S(1)} %collective-permute-done.3), channel_id=1, source_target_pairs={{0,1},{1,2},{2,3},{3,4},{4,5},{5,6},{6,7},{7,8},{8,9},{9,10},{10,1... | collective-permute-start | bytes 393224 | tf_op jit(solution)/shard_map/ppermute | solution.py:17
  43.1 5.1 %collective-permute-start.5 = (bf16[128,512]{1,0:T(8,128)(2,1)S(1)}, bf16[128,512]{1,0:T(8,128)(2,1)S(1)}, u32[]{:S(2)}, u32[]{:S(2)}) collective-permute-start(bf16[128,512]{1,0:T(8,128)(2,1)S(1)} %collective-permute-done.4), channel_id=1, source_target_pairs={{0,1},{1,2},{2,3},{3,4},{4,5},{5,6},{6,7},{7,8},{8,9},{9,10},{10,1... | collective-permute-start | bytes 393224 | tf_op jit(solution)/shard_map/ppermute | solution.py:17
  48.3 4.8 %collective-permute-start.13 = (bf16[128,512]{0,1:T(8,128)(2,1)S(1)}, bf16[128,512]{0,1:T(8,128)(2,1)S(1)}, u32[]{:S(2)}, u32[]{:S(2)}) collective-permute-start(bf16[128,512]{0,1:T(8,128)(2,1)S(1)} %collective-permute-done.12), channel_id=1, source_target_pairs={{0,1},{1,2},{2,3},{3,4},{4,5},{5,6},{6,7},{7,8},{8,9},{9,10},{10,1... | collective-permute-start | bytes 393224 | tf_op jit(solution)/shard_map/ppermute | solution.py:17
  53.1 4.4 %collective-permute-start.6 = (bf16[128,512]{1,0:T(8,128)(2,1)S(1)}, bf16[128,512]{1,0:T(8,128)(2,1)S(1)}, u32[]{:S(2)}, u32[]{:S(2)}) collective-permute-start(bf16[128,512]{1,0:T(8,128)(2,1)S(1)} %collective-permute-done.5), channel_id=1, source_target_pairs={{0,1},{1,2},{2,3},{3,4},{4,5},{5,6},{6,7},{7,8},{8,9},{9,10},{10,1... | collective-permute-start | bytes 393224 | tf_op jit(solution)/shard_map/ppermute | solution.py:17
  58.1 4.9 %collective-permute-start.14 = (bf16[128,512]{0,1:T(8,128)(2,1)S(1)}, bf16[128,512]{0,1:T(8,128)(2,1)}, u32[]{:S(2)}, u32[]{:S(2)}) collective-permute-start(bf16[128,512]{0,1:T(8,128)(2,1)S(1)} %collective-permute-done.13), channel_id=1, source_target_pairs={{0,1},{1,2},{2,3},{3,4},{4,5},{5,6},{6,7},{7,8},{8,9},{9,10},{10,1... | collective-permute-start | bytes 393224 | tf_op jit(solution)/shard_map/ppermute | solution.py:17
  68.3 5.9 %collective-permute-start.15 = (bf16[128,512]{0,1:T(8,128)(2,1)}, bf16[128,512]{0,1:T(8,128)(2,1)}, u32[]{:S(2)}, u32[]{:S(2)}) collective-permute-start(bf16[128,512]{0,1:T(8,128)(2,1)} %collective-permute-done.14), channel_id=1, source_target_pairs={{0,1},{1,2},{2,3},{3,4},{4,5},{5,6},{6,7},{7,8},{8,9},{9,10},{10,1... | collective-permute-start | bytes 393224 | tf_op jit(solution)/shard_map/ppermute | solution.py:17
  81.2 21.8 %while.11 = (s32[]{:T(128)}, bf16[4,128,5,128]{1,3,2,0:T(8,128)(2,1)S(1)}, bf16[4,1152,128]{1,2,0:T(8,128)(2,1)S(1)}, bf16[4,1152,128]{1,2,0:T(8,128)(2,1)}, bf1...) while((s32[]{:T(128)}, ...), condition=%wide.region_3.4_spmd.clone, body=%wide.region_0.3_spmd.clone.sunk | while | flops 573541248 | bytes 1835245 | solution.py:74
  84.1 2.5 fusion.99
  89.6 2.5 fusion.99
  95.0 2.5 fusion.99
  100.5 2.5 fusion.99
  103.0 18.6 %all-gather.2.cloned.1.call-done = bf16[2560,2560]{0,1:T(8,128)(2,1)} async-done(((bf16[2560,80]{0,1:T(8,128)(2,1)}), bf16[2560,2560]{0,1:T(8,128)(2,1)}) %all-gather.2.cloned.1.call-update) | async-done | bytes 13107216 | tf_op jit(solution)/shard_map/all_gather | solution.py:78
  121.6 9.2 %convolution_convert_fusion.2 = bf16[128,2560]{1,0:T(8,128)(2,1)S(1)} fusion(bf16[128,2560]{0,1:T(8,128)(2,1)S(1)} %bitcast.131, bf16[2560,2560]{0,1:T(8,128)(2,1)} %all-gather.2.cloned.1.call-done), kind=kOutput, calls=%fused_computation.35 | convolution fusion | flops 1678049280 | bytes 14417920 | tf_op jit(solution)/shard_map/dot_general | solution.py:76
  135.1 17.4 %all-to-all-start = ((bf16[32,2,4,2560]{3,2,1,0:T(4,128)(2,1)}), bf16[32,2,4,2560]{3,2,1,0:T(4,128)(2,1)S(1)}, u32[]{:S(2)}, u32[]{:S(2)}) async-start(bf16[32,2,4,2560]{3,2,1,0:T(4,128)(2,1)} %reshape_reshape_broadcast_in_dim_reshape.3), calls=%async_computation | async-start | bytes 2621440 | tf_op jit(solution)/shard_map/all_to_all | solution.py:115
  152.5 82.3 %reshape.179 = bf16[2560,2,2,1664]{3,2,1,0:T(2,128)(2,1)} reshape(bf16[2560,2,3328]{2,1,0:T(2,128)(2,1)} %param.20) | data formatting | bytes 68157440 | tf_op jit(solution)/shard_map/reshape | solution.py:109
  236.0 23.3 %fusion.51 = f32[2,2,32,4,1664]{4,2,0,3,1:T(8,128)S(1)} fusion(bf16[2560,2,2,1664,1]{3,2,1,0,4:T(2,128)(2,1)} %bitcast.128, bf16[32,2,4,2560,1]{3,2,1,0,4:T(4,128)(2,1)} %bitcast.129), kind=kOutput, calls=%fused_computation.36 | convolution fusion | flops 4362076160 | bytes 38797312 | tf_op jit(solution)/shard_map/nlkd,dglf->glnkf/dot_general | solution.py:113
  259.3 8.5 %fusion.50 = bf16[32,2,4,2560]{3,0,2,1:T(8,128)(2,1)S(1)} fusion(bf16[2,1664,2560,1]{2,1,3,0:T(8,128)(2,1)} %bitcast.137, f32[2,2,32,4,1664]{4,2,0,3,1:T(8,128)S(1)} %fusion.51), kind=kOutput, calls=%fused_computation.34 | convolution fusion | flops 2184249344 | bytes 21757952 | tf_op jit(solution)/shard_map/lnkf,lfd->nlkd/dot_general | solution.py:120
  269.9 5.7 %all-to-all-start.1 = ((bf16[32,2,4,2560]{3,2,1,0:T(4,128)(2,1)}), bf16[32,2,4,2560]{3,2,1,0:T(4,128)(2,1)S(1)}, u32[]{:S(2)}, u32[]{:S(2)}) async-start(bf16[32,2,4,2560]{3,2,1,0:T(4,128)(2,1)} %copy.109), calls=%async_computation.1 | async-start | bytes 2621440 | tf_op jit(solution)/shard_map/all_to_all | solution.py:124
  275.8 31.7 %all-to-all-done.1 = bf16[32,2,4,2560]{3,2,1,0:T(4,128)(2,1)S(1)} async-done(((bf16[32,2,4,2560]{3,2,1,0:T(4,128)(2,1)}), bf16[32,2,4,2560]{3,2,1,0:T(4,128)(2,1)S(1)}, u32[]{:S(2)}, u32[]{:S(2)}) %all-to-all-start.1) | async-done | bytes 1310752 | tf_op jit(solution)/shard_map/all_to_all | solution.py:124
  (144 shorter events, 46.6 us)
Async XLA Ops:
  7.2 41.1 %copy-start.22 = (s32[128]{0:T(128)S(1)}, s32[128]{0:T(128)}, u32[]{:S(2)}) copy-start(s32[128]{0:T(128)} %param.24) | copy-start | bytes 1540
  7.2 50.3 %copy-start.17 = (s32[128,2]{0,1:T(2,128)S(1)}, s32[128,2]{0,1:T(2,128)}, u32[]{:S(2)}) copy-start(s32[128,2]{0,1:T(2,128)} %param.22) | copy-start | bytes 3076
  7.2 60.0 %copy-start.3 = (bf16[128,2560]{1,0:T(8,128)(2,1)S(1)}, bf16[128,2560]{1,0:T(8,128)(2,1)}, u32[]{:S(2)}) copy-start(bf16[128,2560]{1,0:T(8,128)(2,1)} %param.15) | copy-start | bytes 1966084
  7.2 114.4 %all-gather.2.cloned.1.call-start = ((), (), s32[]{:S(2)}) async-start(), calls=%async_computation.2 | async-start | bytes 13516800 | tf_op jit(solution)/shard_map/all_gather | solution.py:78
  7.9 8.7 %collective-permute-start = (bf16[128,512]{1,0:T(8,128)(2,1)}, bf16[128,512]{1,0:T(8,128)(2,1)S(1)}, u32[]{:S(2)}, u32[]{:S(2)}) collective-permute-start(bf16[128,512]{1,0:T(8,128)(2,1)} %param.17), channel_id=1, source_target_pairs={{0,1},{1,2},{2,3},{3,4},{4,5},{5,6},{6,7},{7,8},{8,9},{9,10},{10,1... | collective-permute-start | bytes 393224 | tf_op jit(solution)/shard_map/ppermute | solution.py:17
  11.4 8.5 %collective-permute-start.8 = (bf16[128,512]{0,1:T(8,128)(2,1)S(1)}, bf16[128,512]{0,1:T(8,128)(2,1)S(1)}, u32[]{:S(2)}, u32[]{:S(2)}) collective-permute-start(bf16[128,512]{0,1:T(8,128)(2,1)S(1)} %copy.92), channel_id=1, source_target_pairs={{0,1},{1,2},{2,3},{3,4},{4,5},{5,6},{6,7},{7,8},{8,9},{9,10},{10,1... | collective-permute-start | bytes 393224 | tf_op jit(solution)/shard_map/ppermute | solution.py:17
  16.6 6.7 %collective-permute-start.1 = (bf16[128,512]{1,0:T(8,128)(2,1)S(1)}, bf16[128,512]{1,0:T(8,128)(2,1)S(1)}, u32[]{:S(2)}, u32[]{:S(2)}) collective-permute-start(bf16[128,512]{1,0:T(8,128)(2,1)S(1)} %collective-permute-done), channel_id=1, source_target_pairs={{0,1},{1,2},{2,3},{3,4},{4,5},{5,6},{6,7},{7,8},{8,9},{9,10},{10,1... | collective-permute-start | bytes 393224 | tf_op jit(solution)/shard_map/ppermute | solution.py:17
  19.9 5.7 %collective-permute-start.9 = (bf16[128,512]{0,1:T(8,128)(2,1)S(1)}, bf16[128,512]{0,1:T(8,128)(2,1)S(1)}, u32[]{:S(2)}, u32[]{:S(2)}) collective-permute-start(bf16[128,512]{0,1:T(8,128)(2,1)S(1)} %collective-permute-done.8), channel_id=1, source_target_pairs={{0,1},{1,2},{2,3},{3,4},{4,5},{5,6},{6,7},{7,8},{8,9},{9,10},{10,1... | collective-permute-start | bytes 393224 | tf_op jit(solution)/shard_map/ppermute | solution.py:17
  23.4 5.8 %collective-permute-start.2 = (bf16[128,512]{1,0:T(8,128)(2,1)S(1)}, bf16[128,512]{1,0:T(8,128)(2,1)S(1)}, u32[]{:S(2)}, u32[]{:S(2)}) collective-permute-start(bf16[128,512]{1,0:T(8,128)(2,1)S(1)} %collective-permute-done.1), channel_id=1, source_target_pairs={{0,1},{1,2},{2,3},{3,4},{4,5},{5,6},{6,7},{7,8},{8,9},{9,10},{10,1... | collective-permute-start | bytes 393224 | tf_op jit(solution)/shard_map/ppermute | solution.py:17
  25.5 8.0 %collective-permute-start.10 = (bf16[128,512]{0,1:T(8,128)(2,1)S(1)}, bf16[128,512]{0,1:T(8,128)(2,1)S(1)}, u32[]{:S(2)}, u32[]{:S(2)}) collective-permute-start(bf16[128,512]{0,1:T(8,128)(2,1)S(1)} %collective-permute-done.9), channel_id=1, source_target_pairs={{0,1},{1,2},{2,3},{3,4},{4,5},{5,6},{6,7},{7,8},{8,9},{9,10},{10,1... | collective-permute-start | bytes 393224 | tf_op jit(solution)/shard_map/ppermute | solution.py:17
  29.2 6.3 %collective-permute-start.3 = (bf16[128,512]{1,0:T(8,128)(2,1)S(1)}, bf16[128,512]{1,0:T(8,128)(2,1)S(1)}, u32[]{:S(2)}, u32[]{:S(2)}) collective-permute-start(bf16[128,512]{1,0:T(8,128)(2,1)S(1)} %collective-permute-done.2), channel_id=1, source_target_pairs={{0,1},{1,2},{2,3},{3,4},{4,5},{5,6},{6,7},{7,8},{8,9},{9,10},{10,1... | collective-permute-start | bytes 393224 | tf_op jit(solution)/shard_map/ppermute | solution.py:17
  33.6 7.6 %collective-permute-start.11 = (bf16[128,512]{0,1:T(8,128)(2,1)S(1)}, bf16[128,512]{0,1:T(8,128)(2,1)S(1)}, u32[]{:S(2)}, u32[]{:S(2)}) collective-permute-start(bf16[128,512]{0,1:T(8,128)(2,1)S(1)} %collective-permute-done.10), channel_id=1, source_target_pairs={{0,1},{1,2},{2,3},{3,4},{4,5},{5,6},{6,7},{7,8},{8,9},{9,10},{10,1... | collective-permute-start | bytes 393224 | tf_op jit(solution)/shard_map/ppermute | solution.py:17
  35.5 7.6 %collective-permute-start.4 = (bf16[128,512]{1,0:T(8,128)(2,1)S(1)}, bf16[128,512]{1,0:T(8,128)(2,1)S(1)}, u32[]{:S(2)}, u32[]{:S(2)}) collective-permute-start(bf16[128,512]{1,0:T(8,128)(2,1)S(1)} %collective-permute-done.3), channel_id=1, source_target_pairs={{0,1},{1,2},{2,3},{3,4},{4,5},{5,6},{6,7},{7,8},{8,9},{9,10},{10,1... | collective-permute-start | bytes 393224 | tf_op jit(solution)/shard_map/ppermute | solution.py:17
  41.1 33.1 %copy-start.14 = (s32[128,2]{0,1:T(2,128)}, s32[128,2]{0,1:T(2,128)S(1)}, u32[]{:S(2)}) copy-start(s32[128,2]{0,1:T(2,128)S(1)} %copy.102) | copy-start | bytes 3076
  41.1 33.1 %copy-start.6 = (bf16[128,512]{0,1:T(8,128)(2,1)}, bf16[128,512]{0,1:T(8,128)(2,1)S(1)}, u32[]{:S(2)}) copy-start(bf16[128,512]{0,1:T(8,128)(2,1)S(1)} %collective-permute-done.11) | copy-start | bytes 393220
  41.2 7.1 %collective-permute-start.12 = (bf16[128,512]{0,1:T(8,128)(2,1)S(1)}, bf16[128,512]{0,1:T(8,128)(2,1)S(1)}, u32[]{:S(2)}, u32[]{:S(2)}) collective-permute-start(bf16[128,512]{0,1:T(8,128)(2,1)S(1)} %collective-permute-done.11), channel_id=1, source_target_pairs={{0,1},{1,2},{2,3},{3,4},{4,5},{5,6},{6,7},{7,8},{8,9},{9,10},{10,1... | collective-permute-start | bytes 393224 | tf_op jit(solution)/shard_map/ppermute | solution.py:17
  43.1 10.0 %collective-permute-start.5 = (bf16[128,512]{1,0:T(8,128)(2,1)S(1)}, bf16[128,512]{1,0:T(8,128)(2,1)S(1)}, u32[]{:S(2)}, u32[]{:S(2)}) collective-permute-start(bf16[128,512]{1,0:T(8,128)(2,1)S(1)} %collective-permute-done.4), channel_id=1, source_target_pairs={{0,1},{1,2},{2,3},{3,4},{4,5},{5,6},{6,7},{7,8},{8,9},{9,10},{10,1... | collective-permute-start | bytes 393224 | tf_op jit(solution)/shard_map/ppermute | solution.py:17
  48.3 9.8 %collective-permute-start.13 = (bf16[128,512]{0,1:T(8,128)(2,1)S(1)}, bf16[128,512]{0,1:T(8,128)(2,1)S(1)}, u32[]{:S(2)}, u32[]{:S(2)}) collective-permute-start(bf16[128,512]{0,1:T(8,128)(2,1)S(1)} %collective-permute-done.12), channel_id=1, source_target_pairs={{0,1},{1,2},{2,3},{3,4},{4,5},{5,6},{6,7},{7,8},{8,9},{9,10},{10,1... | collective-permute-start | bytes 393224 | tf_op jit(solution)/shard_map/ppermute | solution.py:17
  53.1 9.9 %collective-permute-start.6 = (bf16[128,512]{1,0:T(8,128)(2,1)S(1)}, bf16[128,512]{1,0:T(8,128)(2,1)S(1)}, u32[]{:S(2)}, u32[]{:S(2)}) collective-permute-start(bf16[128,512]{1,0:T(8,128)(2,1)S(1)} %collective-permute-done.5), channel_id=1, source_target_pairs={{0,1},{1,2},{2,3},{3,4},{4,5},{5,6},{6,7},{7,8},{8,9},{9,10},{10,1... | collective-permute-start | bytes 393224 | tf_op jit(solution)/shard_map/ppermute | solution.py:17
  58.1 10.1 %collective-permute-start.14 = (bf16[128,512]{0,1:T(8,128)(2,1)S(1)}, bf16[128,512]{0,1:T(8,128)(2,1)}, u32[]{:S(2)}, u32[]{:S(2)}) collective-permute-start(bf16[128,512]{0,1:T(8,128)(2,1)S(1)} %collective-permute-done.13), channel_id=1, source_target_pairs={{0,1},{1,2},{2,3},{3,4},{4,5},{5,6},{6,7},{7,8},{8,9},{9,10},{10,1... | collective-permute-start | bytes 393224 | tf_op jit(solution)/shard_map/ppermute | solution.py:17
  63.0 11.2 %collective-permute-start.7 = (bf16[128,512]{1,0:T(8,128)(2,1)S(1)}, bf16[128,512]{1,0:T(8,128)(2,1)S(1)}, u32[]{:S(2)}, u32[]{:S(2)}) collective-permute-start(bf16[128,512]{1,0:T(8,128)(2,1)S(1)} %collective-permute-done.6), channel_id=1, source_target_pairs={{0,1},{1,2},{2,3},{3,4},{4,5},{5,6},{6,7},{7,8},{8,9},{9,10},{10,1... | collective-permute-start | bytes 393224 | tf_op jit(solution)/shard_map/ppermute | solution.py:17
  68.3 6.9 %collective-permute-start.15 = (bf16[128,512]{0,1:T(8,128)(2,1)}, bf16[128,512]{0,1:T(8,128)(2,1)}, u32[]{:S(2)}, u32[]{:S(2)}) collective-permute-start(bf16[128,512]{0,1:T(8,128)(2,1)} %collective-permute-done.14), channel_id=1, source_target_pairs={{0,1},{1,2},{2,3},{3,4},{4,5},{5,6},{6,7},{7,8},{8,9},{9,10},{10,1... | collective-permute-start | bytes 393224 | tf_op jit(solution)/shard_map/ppermute | solution.py:17
  135.1 99.8 %all-to-all-start = ((bf16[32,2,4,2560]{3,2,1,0:T(4,128)(2,1)}), bf16[32,2,4,2560]{3,2,1,0:T(4,128)(2,1)S(1)}, u32[]{:S(2)}, u32[]{:S(2)}) async-start(bf16[32,2,4,2560]{3,2,1,0:T(4,128)(2,1)} %reshape_reshape_broadcast_in_dim_reshape.3), calls=%async_computation | async-start | bytes 2621440 | tf_op jit(solution)/shard_map/all_to_all | solution.py:115
  269.9 37.6 %all-to-all-start.1 = ((bf16[32,2,4,2560]{3,2,1,0:T(4,128)(2,1)}), bf16[32,2,4,2560]{3,2,1,0:T(4,128)(2,1)S(1)}, u32[]{:S(2)}, u32[]{:S(2)}) async-start(bf16[32,2,4,2560]{3,2,1,0:T(4,128)(2,1)} %copy.109), calls=%async_computation.1 | async-start | bytes 2621440 | tf_op jit(solution)/shard_map/all_to_all | solution.py:124
  (18 other events, 175.4 us)
Sparse Core Ops, SparseCore 0:
  10.9 110.6 all-gather.1
where the time goes:
time: 319 us; the launch traced here: 316 us
  local copies, waits for them, and re-layouts  100 us (31%)
  starting transfers between devices  81.1 us (25%)
  matrix products  61.3 us (19%)
  waiting for transfers between devices  51 us (16%)
  between operations  14.7 us (5%)
  other arithmetic  7.52 us (2%)
    reshape x1, local copies, waits for them, and re-layouts, body(): weights_in = expert_in.reshape(width_d, 2, local_experts, hidden_each)  82.3 us
    ppermute x16, starting transfers between devices, shifted(): lax.ppermute(value, axis, [(source, source + steps) for source in range(i...  58 us
    all_to_all x1, waiting for transfers between devices, body(): lax.all_to_all(computed, 'seq', split_axis=0, concat_axis=0, tiled=True)  31.7 us
    dot_general x1, matrix products, body(): jnp.einsum('nlkd,dglf->glnkf', lax.all_to_all(outgoing, 'seq', split_axis...  23.3 us
    all_gather x1, waiting for transfers between devices, body(): lax.all_gather(out_proj, 'seq', axis=1, tiled=True)  18.6 us
    all_to_all x1, starting transfers between devices, body(): lax.all_to_all(outgoing, 'seq', split_axis=0, concat_axis=0, tiled=True)  17.4 us
    unnamed x66, local copies, waits for them, and re-layouts  10 us
    dot_general x4, matrix products, one_head(): jnp.einsum('gqk,kd->qgd', probs_bf, v_one, preferred_element_type=jnp.flo...  9.93 us
  transfers between devices with their start and end apart: 19, of which 2 were waited for; matrix products, arithmetic and copies ran while one was open for 37% of the time, Pallas kernels for 0%

commit v1 on v0

v1 whole, which is shorter than its diff:
```python
import jax
import jax.numpy as jnp
from jax import lax
from jax.experimental import pallas as pl
from jax.experimental.pallas import tpu as pltpu
from jax.sharding import PartitionSpec as P

HEADS = 20
KV_HEADS = 4
HEAD = 128
WINDOW = 1024
EXPERTS = 64
CAP = 2
SLOTS = 2 * CAP
VMEM_LIMIT = 60 * 1024 * 1024
F32 = jnp.float32
BF16 = jnp.bfloat16
NT = (((1,), (1,)), ((), ()))


def swap(value, mask):
    count = lax.axis_size("seq")
    return lax.ppermute(value, "seq", [(i, i ^ mask) for i in range(count)])


def shift(value, steps):
    count = lax.axis_size("seq")
    return lax.ppermute(value, "seq", [(i, i + steps) for i in range(count - steps)])


def window_blocks(kv, pos, back):
    count = lax.axis_size("seq")
    if back != 8 or count % back:
        found = [(shift(kv, s), pos - s) for s in range(back, 0, -1) if s < count]
        return found + [(kv, pos)]
    group = pos // back
    chip = (pos % back) // 2
    core = pos % 2
    prev = shift(kv, back) if count > back else jnp.zeros_like(kv)
    blocks = [(kv, pos), (prev, pos - back)]
    mate = swap(jnp.where(core == 1, prev, kv), 1)
    blocks.append((mate, jnp.where(core == 0, pos + 1 - back, pos - 1)))
    for m in range(1, back // 2):
        other = chip ^ m
        got = swap(jnp.where(chip < other, kv, prev), 2 * m)
        base = jnp.where(other < chip, group, group - 1) * back + 2 * other
        blocks.append((got, base + core))
        blocks.append((swap(got, 1), base + 1 - core))
    return blocks


def attention_body(count, off_ref, q_ref, *refs):
    k_refs, v_refs, o_ref = refs[:count], refs[count : 2 * count], refs[2 * count]
    rows = q_ref.shape[0]
    group = q_ref.shape[1] // HEAD
    delta = lax.broadcasted_iota(jnp.int32, (rows, rows), 0) - lax.broadcasted_iota(
        jnp.int32, (rows, rows), 1
    )
    bias = []
    for b in range(count):
        d = delta + off_ref[b] * rows
        bias.append(jnp.where((d >= 0) & (d < WINDOW), 0.0, -jnp.inf))
    bias = jnp.concatenate(bias, 1)
    k_all = jnp.concatenate([r[...] for r in k_refs], 0)
    v_all = jnp.concatenate([r[...] for r in v_refs], 0)
    scale = HEAD ** (-0.5) * 1.4426950408889634
    for g in range(group):
        cols = slice(g * HEAD, (g + 1) * HEAD)
        s = lax.dot_general(q_ref[:, cols], k_all, NT, preferred_element_type=F32) + bias
        top = jnp.max(s, -1, keepdims=True)
        w = jnp.exp2((s - top) * scale)
        total = jnp.sum(w, -1, keepdims=True)
        out = jnp.dot(w.astype(BF16), v_all, preferred_element_type=F32)
        o_ref[:, cols] = (out * (1.0 / total)).astype(BF16)


def attention(queries, blocks, offsets):
    rows = queries.shape[0]
    count = len(blocks)
    wide = HEADS // KV_HEADS * HEAD
    k_spec = pl.BlockSpec((rows, HEAD), lambda h: (0, h))
    v_spec = pl.BlockSpec((rows, HEAD), lambda h: (0, h + KV_HEADS))

    def body(*refs):
        attention_body(count, *refs)

    return pl.pallas_call(
        body,
        grid=(KV_HEADS,),
        in_specs=[
            pl.BlockSpec(memory_space=pltpu.SMEM),
            pl.BlockSpec((rows, wide), lambda h: (0, h)),
        ]
        + [k_spec] * count
        + [v_spec] * count,
        out_specs=pl.BlockSpec((rows, wide), lambda h: (0, h)),
        out_shape=jax.ShapeDtypeStruct(queries.shape, BF16),
        compiler_params=pltpu.CompilerParams(vmem_limit_bytes=VMEM_LIMIT),
        name="attention",
    )(offsets, queries, *blocks, *blocks)


def project_body(ctx_ref, w_ref, res_ref, gain_ref, sel_ref, att_ref, slot_ref, hid_ref, sq_ref):
    step = pl.program_id(0)
    att = lax.dot_general(ctx_ref[...], w_ref[...], NT, preferred_element_type=F32).astype(BF16)
    att_ref[...] = att
    hid = res_ref[...].astype(F32) + att.astype(F32)
    hid_ref[step] = hid
    part = jnp.sum(hid * hid, -1, keepdims=True)

    @pl.when(step == 0)
    def _():
        sq_ref[...] = part

    @pl.when(step > 0)
    def _():
        sq_ref[...] += part

    @pl.when(step == pl.num_programs(0) - 1)
    def _():
        width = hid_ref.shape[2]
        total = hid_ref.shape[0] * width
        inv = lax.rsqrt(sq_ref[...] / total + 1e-05)
        for c in range(hid_ref.shape[0]):
            cols = slice(c * width, (c + 1) * width)
            normed = (hid_ref[c] * inv * gain_ref[:, cols]).astype(BF16)
            slot_ref[:, cols] = jnp.dot(
                sel_ref[...], normed, preferred_element_type=F32
            ).astype(BF16)


def project(context, weight_t, residual, gain, select):
    rows, width = residual.shape
    nb = 512
    steps = width // nb
    return pl.pallas_call(
        project_body,
        grid=(steps,),
        in_specs=[
            pl.BlockSpec(context.shape, lambda j: (0, 0)),
            pl.BlockSpec((nb, context.shape[1]), lambda j: (j, 0)),
            pl.BlockSpec((rows, nb), lambda j: (0, j)),
            pl.BlockSpec((1, width), lambda j: (0, 0)),
            pl.BlockSpec(select.shape, lambda j: (0, 0)),
        ],
        out_specs=[
            pl.BlockSpec((rows, nb), lambda j: (0, j)),
            pl.BlockSpec((select.shape[0], width), lambda j: (0, 0)),
        ],
        out_shape=[
            jax.ShapeDtypeStruct((rows, width), BF16),
            jax.ShapeDtypeStruct((select.shape[0], width), BF16),
        ],
        scratch_shapes=[pltpu.VMEM((steps, rows, nb), F32), pltpu.VMEM((rows, 1), F32)],
        compiler_params=pltpu.CompilerParams(vmem_limit_bytes=VMEM_LIMIT),
        name="project",
    )(context, weight_t, residual, gain, select)


def experts_body(local, x_ref, up_hbm, down_hbm, o_ref, up_ref, down_ref, wide_ref, acc_ref, up_sem, down_sem):
    total, width = x_ref.shape
    rows = total // local
    hidden = up_ref.shape[3]
    chunks = up_sem.shape[1]
    depth = width // chunks
    parts = down_sem.shape[1]
    tall = hidden // parts

    def up_copy(e, k):
        return pltpu.make_async_copy(
            up_hbm.at[pl.ds(k * depth, depth), :, pl.ds(e * hidden, hidden)],
            up_ref.at[e, pl.ds(k * depth, depth)],
            up_sem.at[e, k],
        )

    def down_copy(e, k):
        return pltpu.make_async_copy(
            down_hbm.at[pl.ds(e * hidden + k * tall, tall)],
            down_ref.at[e, pl.ds(k * tall, tall)],
            down_sem.at[e, k],
        )

    for e in range(local):
        for k in range(chunks):
            up_copy(e, k).start()
        for k in range(parts):
            down_copy(e, k).start()

    row = lax.broadcasted_iota(jnp.int32, (rows, total), 0)
    col = lax.broadcasted_iota(jnp.int32, (rows, total), 1)
    lane = lax.broadcasted_iota(jnp.int32, (HEAD, 2 * HEAD), 1)
    sub = lax.broadcasted_iota(jnp.int32, (HEAD, 2 * HEAD), 0)
    spread = [jnp.where(lane == 2 * sub + j, 1.0, 0.0).astype(BF16) for j in range(2)]
    per = SLOTS * local
    picks = [
        jnp.where(col == (row // SLOTS) * per + e * SLOTS + row % SLOTS, 1.0, 0.0).astype(BF16)
        for e in range(local)
    ]
    for e in range(local):
        for k in range(chunks):
            mine = jnp.dot(
                picks[e], x_ref[:, k * depth : (k + 1) * depth], preferred_element_type=F32
            ).astype(BF16)
            for c in range(depth // HEAD):
                piece = mine[:, c * HEAD : (c + 1) * HEAD]
                for j in range(2):
                    wide_ref[k, j * rows : (j + 1) * rows, 2 * c * HEAD : 2 * (c + 1) * HEAD] = jnp.dot(
                        piece, spread[j], preferred_element_type=F32
                    ).astype(BF16)

        def up_step(k, carry):
            up_copy(e, k).wait()
            w = up_ref[e, pl.ds(k * depth, depth)].reshape(2 * depth, hidden)
            prod = jnp.dot(wide_ref[k], w, preferred_element_type=F32)

            @pl.when(k == 0)
            def _():
                acc_ref[...] = prod

            @pl.when(k > 0)
            def _():
                acc_ref[...] += prod

            return carry

        lax.fori_loop(0, chunks, up_step, 0)
        gate = acc_ref[:rows]
        act = (gate * jax.nn.sigmoid(gate) * acc_ref[rows:]).astype(BF16)
        for k in range(parts):
            down_copy(e, k).wait()
        out = jnp.dot(act, down_ref[e], preferred_element_type=F32).astype(BF16)
        back = lax.dot_general(
            picks[e], out, (((0,), (0,)), ((), ())), preferred_element_type=F32
        ).astype(BF16)
        if e == 0:
            o_ref[...] = back
        else:
            o_ref[...] = o_ref[...] + back


def experts(x, up, down, local):
    total, width = x.shape
    hidden = up.shape[2] // local
    chunks = 10
    parts = 4
    any_spec = pl.BlockSpec(memory_space=pl.ANY)

    def body(*refs):
        experts_body(local, *refs)

    return pl.pallas_call(
        body,
        in_specs=[pl.BlockSpec(memory_space=pltpu.VMEM), any_spec, any_spec],
        out_specs=pl.BlockSpec(memory_space=pltpu.VMEM),
        out_shape=jax.ShapeDtypeStruct((total, width), BF16),
        scratch_shapes=[
            pltpu.VMEM((local, width, 2, hidden), BF16),
            pltpu.VMEM((local, hidden, width), BF16),
            pltpu.VMEM((chunks, 2 * total // local, 2 * width // chunks), BF16),
            pltpu.VMEM((2 * total // local, hidden), F32),
            pltpu.SemaphoreType.DMA((local, chunks)),
            pltpu.SemaphoreType.DMA((local, parts)),
        ],
        compiler_params=pltpu.CompilerParams(vmem_limit_bytes=VMEM_LIMIT),
        name="experts",
    )(x, up, down)


def experts_plain(x, up, down, local):
    total, width = x.shape
    hidden = up.shape[2] // local
    rows = x.reshape(-1, local, SLOTS, width)
    pair = jnp.einsum(
        "nlkd,dglf->glnkf",
        rows,
        up.reshape(width, 2, local, hidden),
        preferred_element_type=F32,
    )
    act = (jax.nn.silu(pair[0]) * pair[1]).astype(BF16)
    part = jnp.einsum(
        "lnkf,lfd->nlkd", act, down.reshape(local, hidden, width), preferred_element_type=F32
    )
    return part.astype(BF16).reshape(total, width)


def combine_body(high_ref, low_ref, r_ref, o_ref):
    r = r_ref[...]
    o_ref[...] = (
        jnp.dot(high_ref[...], r, preferred_element_type=F32)
        + jnp.dot(low_ref[...], r, preferred_element_type=F32)
    ).astype(BF16)


def combine(high, low, rows):
    width = rows.shape[1]
    nb = 1280
    same = lambda j: (0, 0)
    return pl.pallas_call(
        combine_body,
        grid=(width // nb,),
        in_specs=[
            pl.BlockSpec(high.shape, same),
            pl.BlockSpec(low.shape, same),
            pl.BlockSpec((rows.shape[0], nb), lambda j: (0, j)),
        ],
        out_specs=pl.BlockSpec((high.shape[0], nb), lambda j: (0, j)),
        out_shape=jax.ShapeDtypeStruct((high.shape[0], width), BF16),
        compiler_params=pltpu.CompilerParams(vmem_limit_bytes=VMEM_LIMIT),
        name="combine",
    )(high, low, rows)


def routing(routes, gate_ints, modality, capacity):
    tokens = routes.shape[0]
    key = (routes * 2 + modality[:, None]).reshape(-1)
    order = jnp.arange(2 * tokens, dtype=jnp.int32)
    same = (key[:, None] == key[None, :]) & (order[None, :] < order[:, None])
    rank = jnp.sum(same.astype(jnp.int32), 1)
    hot = key[:, None] == jnp.arange(2 * EXPERTS, dtype=jnp.int32)[None, :]
    limit = jnp.sum(jnp.where(hot, capacity.reshape(1, -1), 0), 1)
    spot = jnp.where(rank < limit, key * CAP + rank, -1).reshape(tokens, 2)
    slot = jnp.arange(EXPERTS * SLOTS, dtype=jnp.int32)
    select = (spot[None, :, 0] == slot[:, None]) | (spot[None, :, 1] == slot[:, None])
    place = spot[:, :, None] == slot[None, None, :]
    low = gate_ints % 8
    high = jnp.sum(jnp.where(place, (gate_ints - low)[:, :, None], 0), 1)
    low = jnp.sum(jnp.where(place, low[:, :, None], 0), 1)
    to_gate = lambda v: (v.astype(F32) / 1024.0).astype(BF16)
    return select.astype(BF16), to_gate(high), to_gate(low)


def body(
    residual,
    queries,
    keys,
    values,
    out_proj,
    norm_gain,
    expert_in,
    expert_down,
    routes,
    gate_ints,
    modality,
    capacity,
):
    devices = lax.axis_size("seq")
    pos = lax.axis_index("seq")
    rows, width = residual.shape
    back = (WINDOW + rows - 1) // rows
    blocks = window_blocks(jnp.concatenate([keys, values], 1), pos, back)
    offsets = jnp.stack([jnp.where(b < 0, 4 * back, pos - b) for _, b in blocks]).astype(jnp.int32)
    weight_t = lax.all_gather(out_proj.T, "seq", axis=0, tiled=True)
    select, high, low = routing(routes, gate_ints, modality, capacity)
    context = attention(queries, [v for v, _ in blocks], offsets)
    attended, slots = project(context, weight_t, residual, norm_gain.reshape(1, width), select)
    ways = max(1, devices // EXPERTS)
    local = max(1, EXPERTS // devices)
    if ways > 1:
        slots = jnp.repeat(slots.reshape(EXPERTS, SLOTS, width), ways, 0)
    outgoing = slots.reshape(devices, local * SLOTS, width)
    arrived = lax.all_to_all(outgoing, "seq", split_axis=0, concat_axis=0, tiled=True)
    arrived = arrived.reshape(devices * local * SLOTS, width)
    if expert_in.shape[2] % (local * HEAD) == 0:
        computed = experts(arrived, expert_in, expert_down, local)
    else:
        computed = experts_plain(arrived, expert_in, expert_down, local)
    computed = lax.optimization_barrier(computed)
    returned = lax.all_to_all(
        computed.reshape(devices, local * SLOTS, width), "seq", split_axis=0, concat_axis=0, tiled=True
    )
    if ways > 1:
        parts = returned.reshape(EXPERTS, ways, SLOTS, width).astype(F32)
        returned = jnp.sum(parts, 1).astype(BF16)
    expert_mix = combine(high, low, returned.reshape(EXPERTS * SLOTS, width))
    return (attended, expert_mix)


def solution(mesh):
    placed = (
        P("seq", None),
        P("seq", None),
        P("seq", None),
        P("seq", None),
        P(None, "seq"),
        P(),
        P(None, None, "seq"),
        P("seq", None),
        P("seq", None),
        P("seq", None),
        P("seq"),
        P(),
    )
    return jax.shard_map(
        body,
        mesh=mesh,
        in_specs=placed,
        out_specs=(P("seq", None), P("seq", None)),
        check_vma=False,
    )
```

time: 319 us -> 234 us (0.73)
  local copies, waits for them, and re-layouts: 100 us -> 7.39 us
  starting transfers between devices: 81.1 us -> 11.8 us
  matrix products: 61.3 us -> 0 us
  waiting for transfers between devices: 51 us -> 108 us
  Pallas kernels: 0 us -> 50.9 us
  blocking collectives: 0 us -> 36.6 us
  other arithmetic: 7.52 us -> 3.45 us
    reshape x2 -> x1, local copies, waits for them, and re-layouts: 82.9 us -> 0.6 us  [body(): norm_gain.reshape(1, width)]
    dot_general x9 -> x0, matrix products: 53 us -> none  [the longest x1 23.3 us: body(): jnp.einsum('nlkd,dglf->glnkf', lax.all_to_all(outgoing, 'seq', split_axis...]
    pallas_call x0 -> x4, Pallas kernels: none -> 50.9 us  [the longest x1 27.4 us: experts(): pl.pallas_call(body, in_specs=[pl.BlockSpec(memory_space=pltpu.VMEM), any...]
    ppermute x16 -> x8, starting transfers between devices: 58 us -> 9.1 us  [the longest x1 4.97 us: shift(): lax.ppermute(value, 'seq', [(i, i + steps) for i in range(count - steps)])]
    all_gather x1, waiting for transfers between devices: 18.6 us -> 61.3 us  [body(): weight_t = lax.all_gather(out_proj.T, 'seq', axis=0, tiled=True)]
    all_to_all x0 -> x1, blocking collectives: none -> 36.6 us  [body(): lax.all_to_all(outgoing, 'seq', split_axis=0, concat_axis=0, tiled=True)]
    all_to_all x2 -> x1, starting transfers between devices: 23.1 us -> 2.68 us  [body(): lax.all_to_all(computed.reshape(devices, local * SLOTS, width), 'seq', sp...]
    ppermute x16 -> x8, waiting for transfers between devices: 0.04 us -> 15.5 us  [the longest x7 12.8 us: swap(): return lax.ppermute(value, 'seq', [(i, i ^ mask) for i in range(count)])]
  transfers between devices with their start and end apart: 19 -> 10, of which waited for: 2 -> 5; matrix products, arithmetic and copies ran while one was open for 37% -> 4% of each run, Pallas kernels for 0% -> 5%
where the time goes in v1:
time: 234 us; the launch traced here: 233 us
  waiting for transfers between devices  108 us (46%)
  Pallas kernels  50.9 us (22%)
  blocking collectives  36.6 us (16%)
  between operations  14.4 us (6%)
  starting transfers between devices  11.8 us (5%)
  local copies, waits for them, and re-layouts  7.39 us (3%)
  other arithmetic  3.45 us (1%)
    all_gather x1, waiting for transfers between devices, body(): weight_t = lax.all_gather(out_proj.T, 'seq', axis=0, tiled=True)  61.3 us
    all_to_all x1, blocking collectives, body(): lax.all_to_all(outgoing, 'seq', split_axis=0, concat_axis=0, tiled=True)  36.6 us
    all_to_all x1, waiting for transfers between devices, body(): lax.all_to_all(computed.reshape(devices, local * SLOTS, width), 'seq', sp...  30.9 us
    pallas_call x1, Pallas kernels, experts(): pl.pallas_call(body, in_specs=[pl.BlockSpec(memory_space=pltpu.VMEM), any...  27.4 us
    ppermute x7, waiting for transfers between devices, swap(): return lax.ppermute(value, 'seq', [(i, i ^ mask) for i in range(count)])  12.8 us
    pallas_call x1, Pallas kernels, attention(): pl.pallas_call(body, grid=(KV_HEADS,), in_specs=[pl.BlockSpec(memory_spac...  10.5 us
    pallas_call x1, Pallas kernels, project(): pl.pallas_call(project_body, grid=(steps,), in_specs=[pl.BlockSpec(contex...  10.5 us
    ppermute x1, starting transfers between devices, shift(): lax.ppermute(value, 'seq', [(i, i + steps) for i in range(count - steps)])  4.97 us
  transfers between devices with their start and end apart: 10, of which 5 were waited for; matrix products, arithmetic and copies ran while one was open for 4% of the time, Pallas kernels for 5%

profile of v1, /device:TPU:0, one launch (start us, length us, event | category | flops | bytes accessed | tf_op | source)
XLA Modules:
  0.0 233.0 jit_solution(3107567380269526392)
XLA Ops:
  7.2 0.7 all-gather.2.cloned.1.call-update
  7.9 0.9 constant_dynamic-update-slice_fusion.1
  8.8 0.9 constant_dynamic-update-slice_fusion.refs_2_.refs_11_
  9.8 5.0 %collective-permute-start = (bf16[128,1024]{1,0:T(8,128)(2,1)S(1)}, bf16[128,1024]{1,0:T(8,128)(2,1)S(1)}, u32[]{:S(2)}, u32[]{:S(2)}) collective-permute-start(bf16[128,1024]{1,0:T(8,128)(2,1)S(1)} %constant_dynamic-update-slice_fusion.refs_2_.refs_11_), channel_id=1, source_target_pairs={{0,8},{1,9},{2,10},{3,11},{4,12},{5,13},{6,14},{7,15},{8,16},{9,17... | collective-permute-start | bytes 786440 | tf_op jit(solution)/shard_map/ppermute | solution.py:28
  14.8 0.7 broadcast_multiply_fusion
  15.6 0.7 broadcast_add_fusion
  16.5 0.8 copy.30
  17.6 2.7 %collective-permute-done.refs_3_.refs_12_ = bf16[128,1024]{1,0:T(8,128)(2,1)S(1)} collective-permute-done((bf16[128,1024]{1,0:T(8,128)(2,1)S(1)}, bf16[128,1024]{1,0:T(8,128)(2,1)S(1)}, u32[]{:S(2)}, u32[]{:S(2)}) %collective-permute-start) | collective-permute-done | bytes 262176 | tf_op jit(solution)/shard_map/ppermute | solution.py:28
  20.4 1.6 collective-permute-start.2
  21.9 1.5 collective-permute-start.4
  24.6 8.0 %collective-permute-done.2.refs_5_.refs_14_ = bf16[128,1024]{1,0:T(8,128)(2,1)S(1)} collective-permute-done((bf16[128,1024]{1,0:T(8,128)(2,1)S(1)}, bf16[128,1024]{1,0:T(8,128)(2,1)S(1)}, u32[]{:S(2)}, u32[]{:S(2)}) %collective-permute-start.2) | collective-permute-done | bytes 262176 | tf_op jit(solution)/shard_map/ppermute | solution.py:23
  32.5 4.8 %collective-permute-done.4.refs_7_.refs_16_ = bf16[128,1024]{1,0:T(8,128)(2,1)S(1)} collective-permute-done((bf16[128,1024]{1,0:T(8,128)(2,1)S(1)}, bf16[128,1024]{1,0:T(8,128)(2,1)S(1)}, u32[]{:S(2)}, u32[]{:S(2)}) %collective-permute-start.4) | collective-permute-done | bytes 262176 | tf_op jit(solution)/shard_map/ppermute | solution.py:23
  39.4 0.6 fusion.2.sel_ref
  40.9 0.7 copy-done.9
  41.7 10.5 %attention.1.ctx_ref = bf16[128,2560]{1,0:T(8,128)(2,1)} custom-call(s32[9]{0:T(128)} %stack.39.refs_0_, bf16[128,2560]{1,0:T(8,128)(2,1)} %refs_1_.2, bf16[128,1024]{1,0:T(8,128)(2,1)} %copy-done.1, bf16[128,1024]{1,0:T(8,128)(2,1)} %copy-done.2, bf16[128,1024]{1,0:T(8,128)(2,1)} %copy-done.6, bf16[128,1024]{1,0:T(8,128)(2,1)} %copy-done.3, ...), custom_call_target="tpu_custom_call" | custom-call | tf_op jit(solution)/shard_map/attention/pallas_call | solution.py:87
  52.2 61.3 %all-gather.2.cloned.1.call-done.w_ref = bf16[2560,2560]{1,0:T(8,128)(2,1)} async-done(((bf16[80,2560]{1,0:T(8,128)(2,1)}), bf16[2560,2560]{1,0:T(8,128)(2,1)}) %all-gather.2.cloned.1.call-update) | async-done | bytes 13107216 | tf_op jit(solution)/shard_map/all_gather | solution.py:352
  113.5 10.5 %project.1 = (bf16[128,2560]{1,0:T(8,128)(2,1)}, bf16[256,2560]{1,0:T(8,128)(2,1)}) custom-call(bf16[128,2560]{1,0:T(8,128)(2,1)} %attention.1.ctx_ref, bf16[2560,2560]{1,0:T(8,128)(2,1)} %all-gather.2.cloned.1.call-done.w_ref, bf16[128,2560]{1,0:T(8,128)(2,1)} %res_ref.1, f32[1,2560]{1,0:T(1,128)} %reshape.43.gain_ref, bf16[256,128]{1,0:T(8,128)(2,1)} %fusion.2.sel_ref), custom_call_target="tpu_custom_call" | custom-call | tf_op jit(solution)/shard_map/project/pallas_call | solution.py:136
  124.0 36.6 %all_to_all.10 = bf16[32,8,2560]{2,1,0:T(8,128)(2,1)} all-to-all(bf16[32,8,2560]{2,1,0:T(8,128)(2,1)} %bitcast.17), channel_id=1, replica_groups=mesh['seq'=32] {'seq'}, dimensions={0} | all-to-all | bytes 2621440 | tf_op jit(solution)/shard_map/all_to_all | solution.py:361
  160.6 27.4 %experts.1 = bf16[256,2560]{1,0:T(8,128)(2,1)} custom-call(bf16[256,2560]{1,0:T(8,128)(2,1)} %bitcast.15, bf16[2560,2,3328]{2,1,0:T(2,128)(2,1)} %refs_1_.3, bf16[3328,2560]{1,0:T(8,128)(2,1)} %refs_2_.1), custom_call_target="tpu_custom_call" | custom-call | tf_op jit(solution)/shard_map/experts/pallas_call | solution.py:251
  188.0 2.7 %all-to-all-start.1 = ((bf16[32,8,2560]{2,1,0:T(8,128)(2,1)}), bf16[32,8,2560]{2,1,0:T(8,128)(2,1)S(1)}, u32[]{:S(2)}, u32[]{:S(2)}) async-start(bf16[32,8,2560]{2,1,0:T(8,128)(2,1)} %bitcast.14), calls=%async_computation.1 | async-start | bytes 2621440 | tf_op jit(solution)/shard_map/all_to_all | solution.py:368
  191.0 0.7 multiply_convert_fusion
  191.7 30.9 %all-to-all-done.1 = bf16[32,8,2560]{2,1,0:T(8,128)(2,1)S(1)} async-done(((bf16[32,8,2560]{2,1,0:T(8,128)(2,1)}), bf16[32,8,2560]{2,1,0:T(8,128)(2,1)S(1)}, u32[]{:S(2)}, u32[]{:S(2)}) %all-to-all-start.1) | async-done | bytes 1310752 | tf_op jit(solution)/shard_map/all_to_all | solution.py:368
  222.6 1.1 copy-done
  223.7 2.5 %combine.1 = bf16[128,2560]{1,0:T(8,128)(2,1)} custom-call(bf16[128,256]{1,0:T(8,128)(2,1)} %get-tuple-element.17.high_ref, bf16[128,256]{1,0:T(8,128)(2,1)} %get-tuple-element.16.low_ref, bf16[256,2560]{1,0:T(8,128)(2,1)} %bitcast.16), custom_call_target="tpu_custom_call" | custom-call | tf_op jit(solution)/shard_map/combine/pallas_call | solution.py:298
  (50 shorter events, 4.8 us)
Async XLA Ops:
  7.2 106.4 %all-gather.2.cloned.1.call-start = ((), (), s32[]{:S(2)}) async-start(), calls=%async_computation.2 | async-start | bytes 13516800 | tf_op jit(solution)/shard_map/all_gather | solution.py:352
  7.9 16.5 %copy-start.11 = (s32[128]{0:T(128)S(1)}, s32[128]{0:T(128)}, u32[]{:S(2)}) copy-start(s32[128]{0:T(128)} %param.22) | copy-start | bytes 1540
  9.8 28.4 %copy-start.1 = (bf16[128,1024]{1,0:T(8,128)(2,1)}, bf16[128,1024]{1,0:T(8,128)(2,1)S(1)}, u32[]{:S(2)}) copy-start(bf16[128,1024]{1,0:T(8,128)(2,1)S(1)} %constant_dynamic-update-slice_fusion.refs_2_.refs_11_) | copy-start | bytes 786436
  9.8 10.5 %collective-permute-start = (bf16[128,1024]{1,0:T(8,128)(2,1)S(1)}, bf16[128,1024]{1,0:T(8,128)(2,1)S(1)}, u32[]{:S(2)}, u32[]{:S(2)}) collective-permute-start(bf16[128,1024]{1,0:T(8,128)(2,1)S(1)} %constant_dynamic-update-slice_fusion.refs_2_.refs_11_), channel_id=1, source_target_pairs={{0,8},{1,9},{2,10},{3,11},{4,12},{5,13},{6,14},{7,15},{8,16},{9,17... | collective-permute-start | bytes 786440 | tf_op jit(solution)/shard_map/ppermute | solution.py:28
  14.8 23.4 %copy-start.10 = (f32[2560]{0:T(1024)S(1)}, f32[2560]{0:T(1024)}, u32[]{:S(2)}) copy-start(f32[2560]{0:T(1024)} %param.17) | copy-start | bytes 30724
  20.3 19.8 %copy-start.2 = (bf16[128,1024]{1,0:T(8,128)(2,1)}, bf16[128,1024]{1,0:T(8,128)(2,1)S(1)}, u32[]{:S(2)}) copy-start(bf16[128,1024]{1,0:T(8,128)(2,1)S(1)} %collective-permute-done.refs_3_.refs_12_) | copy-start | bytes 786436
  20.4 12.2 %collective-permute-start.2 = (bf16[128,1024]{1,0:T(8,128)(2,1)S(1)}, bf16[128,1024]{1,0:T(8,128)(2,1)S(1)}, u32[]{:S(2)}, u32[]{:S(2)}) collective-permute-start(bf16[128,1024]{1,0:T(8,128)(2,1)S(1)} %get-tuple-element.14), channel_id=1, source_target_pairs={{0,2},{1,3},{2,0},{3,1},{4,6},{5,7},{6,4},{7,5},{8,10},{9,11},{10,... | collective-permute-start | bytes 786440 | tf_op jit(solution)/shard_map/ppermute | solution.py:23
  21.9 15.4 %collective-permute-start.4 = (bf16[128,1024]{1,0:T(8,128)(2,1)S(1)}, bf16[128,1024]{1,0:T(8,128)(2,1)S(1)}, u32[]{:S(2)}, u32[]{:S(2)}) collective-permute-start(bf16[128,1024]{1,0:T(8,128)(2,1)S(1)} %get-tuple-element.13), channel_id=1, source_target_pairs={{0,4},{1,5},{2,6},{3,7},{4,0},{5,1},{6,2},{7,3},{8,12},{9,13},{10,... | collective-permute-start | bytes 786440 | tf_op jit(solution)/shard_map/ppermute | solution.py:23
  23.4 13.9 %collective-permute-start.6 = (bf16[128,1024]{1,0:T(8,128)(2,1)S(1)}, bf16[128,1024]{1,0:T(8,128)(2,1)S(1)}, u32[]{:S(2)}, u32[]{:S(2)}) collective-permute-start(bf16[128,1024]{1,0:T(8,128)(2,1)S(1)} %get-tuple-element.12), channel_id=1, source_target_pairs={{0,6},{1,7},{2,4},{3,5},{4,2},{5,3},{6,0},{7,1},{8,14},{9,15},{10,... | collective-permute-start | bytes 786440 | tf_op jit(solution)/shard_map/ppermute | solution.py:23
  24.5 15.6 %collective-permute-start.1 = (bf16[128,1024]{1,0:T(8,128)(2,1)S(1)}, bf16[128,1024]{1,0:T(8,128)(2,1)S(1)}, u32[]{:S(2)}, u32[]{:S(2)}) collective-permute-start(bf16[128,1024]{1,0:T(8,128)(2,1)S(1)} %get-tuple-element.15), channel_id=1, source_target_pairs={{0,1},{1,0},{2,3},{3,2},{4,5},{5,4},{6,7},{7,6},{8,9},{9,8},{10,11... | collective-permute-start | bytes 786440 | tf_op jit(solution)/shard_map/ppermute | solution.py:23
  32.5 7.6 %copy-start.3 = (bf16[128,1024]{1,0:T(8,128)(2,1)}, bf16[128,1024]{1,0:T(8,128)(2,1)S(1)}, u32[]{:S(2)}) copy-start(bf16[128,1024]{1,0:T(8,128)(2,1)S(1)} %collective-permute-done.2.refs_5_.refs_14_) | copy-start | bytes 786436
  32.5 7.5 %collective-permute-start.3 = (bf16[128,1024]{1,0:T(8,128)(2,1)S(1)}, bf16[128,1024]{1,0:T(8,128)(2,1)S(1)}, u32[]{:S(2)}, u32[]{:S(2)}) collective-permute-start(bf16[128,1024]{1,0:T(8,128)(2,1)S(1)} %collective-permute-done.2.refs_5_.refs_14_), channel_id=1, source_target_pairs={{0,1},{1,0},{2,3},{3,2},{4,5},{5,4},{6,7},{7,6},{8,9},{9,8},{10,11... | collective-permute-start | bytes 786440 | tf_op jit(solution)/shard_map/ppermute | solution.py:23
  37.4 2.7 %copy-start.4 = (bf16[128,1024]{1,0:T(8,128)(2,1)}, bf16[128,1024]{1,0:T(8,128)(2,1)S(1)}, u32[]{:S(2)}) copy-start(bf16[128,1024]{1,0:T(8,128)(2,1)S(1)} %collective-permute-done.4.refs_7_.refs_16_) | copy-start | bytes 786436
  37.4 2.7 %collective-permute-start.5 = (bf16[128,1024]{1,0:T(8,128)(2,1)S(1)}, bf16[128,1024]{1,0:T(8,128)(2,1)S(1)}, u32[]{:S(2)}, u32[]{:S(2)}) collective-permute-start(bf16[128,1024]{1,0:T(8,128)(2,1)S(1)} %collective-permute-done.4.refs_7_.refs_16_), channel_id=1, source_target_pairs={{0,1},{1,0},{2,3},{3,2},{4,5},{5,4},{6,7},{7,6},{8,9},{9,8},{10,11... | collective-permute-start | bytes 786440 | tf_op jit(solution)/shard_map/ppermute | solution.py:23
  37.4 2.7 %copy-start.5 = (bf16[128,1024]{1,0:T(8,128)(2,1)}, bf16[128,1024]{1,0:T(8,128)(2,1)S(1)}, u32[]{:S(2)}) copy-start(bf16[128,1024]{1,0:T(8,128)(2,1)S(1)} %collective-permute-done.6.refs_9_.refs_18_) | copy-start | bytes 786436
  37.4 2.7 %collective-permute-start.7 = (bf16[128,1024]{1,0:T(8,128)(2,1)S(1)}, bf16[128,1024]{1,0:T(8,128)(2,1)S(1)}, u32[]{:S(2)}, u32[]{:S(2)}) collective-permute-start(bf16[128,1024]{1,0:T(8,128)(2,1)S(1)} %collective-permute-done.6.refs_9_.refs_18_), channel_id=1, source_target_pairs={{0,1},{1,0},{2,3},{3,2},{4,5},{5,4},{6,7},{7,6},{8,9},{9,8},{10,11... | collective-permute-start | bytes 786440 | tf_op jit(solution)/shard_map/ppermute | solution.py:23
  40.0 0.7 copy-start.6
  40.0 0.8 copy-start.7
  40.1 0.9 copy-start.8
  40.9 0.7 copy-start.9
  188.0 2.8 %copy-start.12 = (s32[128,2]{0,1:T(2,128)S(1)}, s32[128,2]{0,1:T(2,128)}, u32[]{:S(2)}) copy-start(s32[128,2]{0,1:T(2,128)} %param.21) | copy-start | bytes 3076
  188.0 34.6 %all-to-all-start.1 = ((bf16[32,8,2560]{2,1,0:T(8,128)(2,1)}), bf16[32,8,2560]{2,1,0:T(8,128)(2,1)S(1)}, u32[]{:S(2)}, u32[]{:S(2)}) async-start(bf16[32,8,2560]{2,1,0:T(8,128)(2,1)} %bitcast.14), calls=%async_computation.1 | async-start | bytes 2621440 | tf_op jit(solution)/shard_map/all_to_all | solution.py:368
  222.6 1.1 copy-start
Sparse Core Ops, SparseCore 0:
  10.8 102.6 all-gather.1

commit v2 on v1

--- a/solution.py
+++ b/solution.py
@@ -4,6 +4,7 @@
 from jax.experimental import pallas as pl
 from jax.experimental.pallas import tpu as pltpu
 from jax.sharding import PartitionSpec as P
+
 
 HEADS = 20
 KV_HEADS = 4
@@ -157,6 +158,133 @@
     )(context, weight_t, residual, gain, select)
 
 
+def gather_weight(own, back):
+    count = lax.axis_size("seq")
+    groups = count // back
+    rows = own.shape[0]
+    cut = rows // 32 * 16 + 16
+    turn = [(i, (i + back) % count) for i in range(count)]
+
+    def onward(value):
+        return lax.ppermute(value, "seq", turn)
+
+    x, y = swap(own, 2), swap(own, 4)
+    far = jnp.concatenate([swap(y[:cut], 2), swap(x[cut:], 4)], 0)
+    found = [[own, x, y, far]]
+    for _ in range(1, groups):
+        own = onward(own)
+        far = onward(far)
+        found.append([own, swap(own, 2), swap(own, 4), far])
+    return found
+
+
+def half_body(groups, where_ref, mine_ref, other_ref, *refs):
+    bufs = refs[: 4 * groups]
+    keep_ref, send_ref, w_ref, sem = refs[4 * groups :]
+    tall = w_ref.shape[1]
+    group, chip = where_ref[0], where_ref[1]
+    rows = bufs[0].shape[0]
+    used = 4 * rows
+
+    def copies(s):
+        slot = lax.rem(group - s + groups, groups)
+        for m in range(4):
+            to = pl.multiple_of((chip ^ m) * rows, 16)
+            yield pltpu.make_async_copy(
+                bufs[4 * s + m], w_ref.at[slot, pl.ds(to, rows)], sem.at[s, m]
+            )
+
+    for s in range(groups):
+        for c in copies(s):
+            c.start()
+    for s in range(groups):
+        w_ref[s, used:] = jnp.zeros((tall - used, w_ref.shape[2]), BF16)
+    both = jnp.concatenate([mine_ref[...], other_ref[...]], 0)
+    half = mine_ref.shape[0]
+    for s in range(groups):
+        for c in copies(s):
+            c.wait()
+        slot = lax.rem(group - s + groups, groups)
+        out = lax.dot_general(both, w_ref[slot], NT, preferred_element_type=F32).astype(BF16)
+        keep_ref[slot] = out[:half]
+        send_ref[slot] = out[half:]
+
+
+def project_half(where, mine, other, found):
+    groups = len(found)
+    bufs = [b for row in found for b in row]
+    tall = -(-4 * bufs[0].shape[0] // HEAD) * HEAD
+    tokens, width = mine.shape
+    shape = jax.ShapeDtypeStruct((groups, tokens, tall), BF16)
+
+    def body(*refs):
+        half_body(groups, *refs)
+
+    vmem = pl.BlockSpec(memory_space=pltpu.VMEM)
+    return pl.pallas_call(
+        body,
+        in_specs=[pl.BlockSpec(memory_space=pltpu.SMEM), vmem, vmem]
+        + [pl.BlockSpec(memory_space=pltpu.HBM)] * len(bufs),
+        out_specs=[vmem, vmem],
+        out_shape=[shape, shape],
+        scratch_shapes=[
+            pltpu.VMEM((groups, tall, width), BF16),
+            pltpu.SemaphoreType.DMA((groups, 4)),
+        ],
+        compiler_params=pltpu.CompilerParams(vmem_limit_bytes=VMEM_LIMIT),
+        name="project_half",
+    )(where, mine, other, *bufs)
+
+
+def merge_body(rows, where_ref, mine_ref, their_ref, res_ref, gain_ref, sel_ref, att_ref, slot_ref, hid_ref):
+    groups, tokens, tall = mine_ref.shape
+    wide = 8 * rows
+    core = where_ref[2]
+    line = lax.broadcasted_iota(jnp.int32, (tall, wide), 0)
+    col = lax.broadcasted_iota(jnp.int32, (tall, wide), 1)
+    pair, rest = col // (2 * rows), col % (2 * rows)
+    side = jnp.where(rest >= rows, 1, 0)
+    hit = line == pair * rows + rest - side * rows
+    pick_mine = jnp.where(hit & (side == core), 1.0, 0.0).astype(BF16)
+    pick_their = jnp.where(hit & (side != core), 1.0, 0.0).astype(BF16)
+    square = jnp.zeros((tokens, 1), F32)
+    for g in range(groups):
+        cols = slice(g * wide, (g + 1) * wide)
+        att = jnp.dot(mine_ref[g], pick_mine, preferred_element_type=F32) + jnp.dot(
+            their_ref[g], pick_their, preferred_element_type=F32
+        )
+        att_ref[:, cols] = att.astype(BF16)
+        hid = res_ref[:, cols].astype(F32) + att
+        hid_ref[:, cols] = hid
+        square += jnp.sum(hid * hid, -1, keepdims=True)
+    inv = lax.rsqrt(square / (groups * wide) + 1e-05)
+    for g in range(groups):
+        cols = slice(g * wide, (g + 1) * wide)
+        normed = (hid_ref[:, cols] * inv * gain_ref[:, cols]).astype(BF16)
+        slot_ref[:, cols] = jnp.dot(sel_ref[...], normed, preferred_element_type=F32).astype(BF16)
+
+
+def merge(where, mine, theirs, residual, gain, select, rows):
+    tokens, width = residual.shape
+    vmem = pl.BlockSpec(memory_space=pltpu.VMEM)
+
+    def body(*refs):
+        merge_body(rows, *refs)
+
+    return pl.pallas_call(
+        body,
+        in_specs=[pl.BlockSpec(memory_space=pltpu.SMEM)] + [vmem] * 5,
+        out_specs=[vmem, vmem],
+        out_shape=[
+            jax.ShapeDtypeStruct((tokens, width), BF16),
+            jax.ShapeDtypeStruct((select.shape[0], width), BF16),
+        ],
+        scratch_shapes=[pltpu.VMEM((tokens, width), F32)],
+        compiler_params=pltpu.CompilerParams(vmem_limit_bytes=VMEM_LIMIT),
+        name="merge",
+    )(where, mine, theirs, residual, gain, select)
+
+
 def experts_body(local, x_ref, up_hbm, down_hbm, o_ref, up_ref, down_ref, wide_ref, acc_ref, up_sem, down_sem):
     total, width = x_ref.shape
     rows = total // local
@@ -208,22 +336,14 @@
                         piece, spread[j], preferred_element_type=F32
                     ).astype(BF16)
 
-        def up_step(k, carry):
+        for k in range(chunks):
             up_copy(e, k).wait()
             w = up_ref[e, pl.ds(k * depth, depth)].reshape(2 * depth, hidden)
             prod = jnp.dot(wide_ref[k], w, preferred_element_type=F32)
-
-            @pl.when(k == 0)
-            def _():
+            if k == 0:
                 acc_ref[...] = prod
-
-            @pl.when(k > 0)
-            def _():
+            else:
                 acc_ref[...] += prod
-
-            return carry
-
-        lax.fori_loop(0, chunks, up_step, 0)
         gate = acc_ref[:rows]
         act = (gate * jax.nn.sigmoid(gate) * acc_ref[rows:]).astype(BF16)
         for k in range(parts):
@@ -241,7 +361,7 @@
 def experts(x, up, down, local):
     total, width = x.shape
     hidden = up.shape[2] // local
-    chunks = 10
+    chunks = 5
     parts = 4
     any_spec = pl.BlockSpec(memory_space=pl.ANY)
 
@@ -349,10 +469,19 @@
     back = (WINDOW + rows - 1) // rows
     blocks = window_blocks(jnp.concatenate([keys, values], 1), pos, back)
     offsets = jnp.stack([jnp.where(b < 0, 4 * back, pos - b) for _, b in blocks]).astype(jnp.int32)
-    weight_t = lax.all_gather(out_proj.T, "seq", axis=0, tiled=True)
     select, high, low = routing(routes, gate_ints, modality, capacity)
-    context = attention(queries, [v for v, _ in blocks], offsets)
-    attended, slots = project(context, weight_t, residual, norm_gain.reshape(1, width), select)
+    gain = norm_gain.reshape(1, width)
+    shard = out_proj.shape[1]
+    if back == 8 and devices % back == 0 and shard % 16 == 0 and back * shard % HEAD == 0:
+        found = gather_weight(out_proj.T, back)
+        where = jnp.stack([pos // back, pos % back // 2, pos % 2]).astype(jnp.int32)
+        context = attention(queries, [v for v, _ in blocks], offsets)
+        mine, send = project_half(where, context, swap(context, 1), found)
+        attended, slots = merge(where, mine, swap(send, 1), residual, gain, select, shard)
+    else:
+        weight_t = lax.all_gather(out_proj.T, "seq", axis=0, tiled=True)
+        context = attention(queries, [v for v, _ in blocks], offsets)
+        attended, slots = project(context, weight_t, residual, gain, select)
     ways = max(1, devices // EXPERTS)
     local = max(1, EXPERTS // devices)
     if ways > 1:

time: 234 us -> 198 us (0.85)
  waiting for transfers between devices: 108 us -> 72 us
  starting transfers between devices: 11.8 us -> 29.9 us
  between operations: 14.4 us -> 1.03 us
  Pallas kernels: 50.9 us -> 46 us
    all_gather x1 -> x0, waiting for transfers between devices: 61.3 us -> none  [body(): weight_t = lax.all_gather(out_proj.T, 'seq', axis=0, tiled=True)]
    ppermute x7 -> x19, waiting for transfers between devices: 12.8 us -> 30.4 us  [swap(): return lax.ppermute(value, 'seq', [(i, i ^ mask) for i in range(count)])]
    ppermute x7 -> x19, starting transfers between devices: 4.13 us -> 18.2 us  [swap(): return lax.ppermute(value, 'seq', [(i, i ^ mask) for i in range(count)])]
    ppermute x0 -> x6, waiting for transfers between devices: none -> 10.1 us  [onward(): return lax.ppermute(value, 'seq', turn)]
    pallas_call x1, Pallas kernels: 27.4 us -> 21.7 us  [experts(): pl.pallas_call(body, in_specs=[pl.BlockSpec(memory_space=pltpu.VMEM), any...]
    ppermute x0 -> x6, starting transfers between devices: none -> 5.52 us  [onward(): return lax.ppermute(value, 'seq', turn)]
    pallas_call x1 -> x2, Pallas kernels: 10.5 us -> 11.3 us  [the longest x1 7.13 us: project_half(): pl.pallas_call(body, in_specs=[pl.BlockSpec(memory_space=pltpu.SMEM), vme...]
  transfers between devices with their start and end apart: 10 -> 27, of which waited for: 5 -> 14; matrix products, arithmetic and copies ran while one was open for 4% -> 3% of each run, Pallas kernels for 5% -> 5%
where the time goes in v2:
time: 198 us; the launch traced here: 197 us
  waiting for transfers between devices  72 us (36%)
  Pallas kernels  46 us (23%)
  blocking collectives  38.8 us (20%)
  starting transfers between devices  29.9 us (15%)
  local copies, waits for them, and re-layouts  6.75 us (3%)
  other arithmetic  2.75 us (1%)
    all_to_all x1, blocking collectives, body(): lax.all_to_all(outgoing, 'seq', split_axis=0, concat_axis=0, tiled=True)  38.8 us
    all_to_all x1, waiting for transfers between devices, body(): lax.all_to_all(computed.reshape(devices, local * SLOTS, width), 'seq', sp...  30.9 us
    ppermute x19, waiting for transfers between devices, swap(): return lax.ppermute(value, 'seq', [(i, i ^ mask) for i in range(count)])  30.4 us
    pallas_call x1, Pallas kernels, experts(): pl.pallas_call(body, in_specs=[pl.BlockSpec(memory_space=pltpu.VMEM), any...  21.7 us
    ppermute x19, starting transfers between devices, swap(): return lax.ppermute(value, 'seq', [(i, i ^ mask) for i in range(count)])  18.2 us
    pallas_call x1, Pallas kernels, attention(): pl.pallas_call(body, grid=(KV_HEADS,), in_specs=[pl.BlockSpec(memory_spac...  10.6 us
    ppermute x6, waiting for transfers between devices, onward(): return lax.ppermute(value, 'seq', turn)  10.1 us
    pallas_call x1, Pallas kernels, project_half(): pl.pallas_call(body, in_specs=[pl.BlockSpec(memory_space=pltpu.SMEM), vme...  7.13 us
  transfers between devices with their start and end apart: 27, of which 14 were waited for; matrix products, arithmetic and copies ran while one was open for 3% of the time, Pallas kernels for 5%

profile of v2, /device:TPU:0, one launch (start us, length us, event | category | flops | bytes accessed | tf_op | source)
XLA Modules:
  0.0 197.3 jit_solution(8574689713128855092)
XLA Ops:
  0.6 3.1 %collective-permute-start.10 = (bf16[80,2560]{1,0:T(8,128)(2,1)}, bf16[80,2560]{1,0:T(8,128)(2,1)S(1)}, u32[]{:S(2)}, u32[]{:S(2)}) collective-permute-start(bf16[80,2560]{1,0:T(8,128)(2,1)} %bitcast.21), channel_id=1, source_target_pairs={{0,4},{1,5},{2,6},{3,7},{4,0},{5,1},{6,2},{7,3},{8,12},{9,13},{10,... | collective-permute-start | bytes 1228808 | tf_op jit(solution)/shard_map/ppermute | solution.py:24
  5.5 3.5 %collective-permute-start = (bf16[128,1024]{1,0:T(8,128)(2,1)S(1)}, bf16[128,1024]{1,0:T(8,128)(2,1)S(1)}, u32[]{:S(2)}, u32[]{:S(2)}) collective-permute-start(bf16[128,1024]{1,0:T(8,128)(2,1)S(1)} %constant_dynamic-update-slice_fusion.refs_2_.refs_11_), channel_id=1, source_target_pairs={{0,8},{1,9},{2,10},{3,11},{4,12},{5,13},{6,14},{7,15},{8,16},{9,17... | collective-permute-start | bytes 786440 | tf_op jit(solution)/shard_map/ppermute | solution.py:29
  9.0 1.6 collective-permute-start.9
  10.6 1.6 collective-permute-start.13
  13.4 1.8 collective-permute-start.11
  15.8 1.6 collective-permute-start.2
  17.8 3.8 %collective-permute-done.9.refs_4_ = bf16[80,2560]{1,0:T(8,128)(2,1)S(1)} collective-permute-done((bf16[80,2560]{1,0:T(8,128)(2,1)}, bf16[80,2560]{1,0:T(8,128)(2,1)S(1)}, u32[]{:S(2)}, u32[]{:S(2)}) %collective-permute-start.9) | collective-permute-done | bytes 409632 | tf_op jit(solution)/shard_map/ppermute | solution.py:24
  23.1 3.8 %collective-permute-done.11 = bf16[48,2560]{1,0:T(8,128)(2,1)S(1)} collective-permute-done((bf16[48,2560]{1,0:T(8,128)(2,1)S(1)}, bf16[48,2560]{1,0:T(8,128)(2,1)S(1)}, u32[]{:S(2)}, u32[]{:S(2)}) %collective-permute-start.11) | collective-permute-done | bytes 245792 | tf_op jit(solution)/shard_map/ppermute | solution.py:24
  27.6 5.0 %collective-permute-done.2.refs_5_.refs_14_ = bf16[128,1024]{1,0:T(8,128)(2,1)S(1)} collective-permute-done((bf16[128,1024]{1,0:T(8,128)(2,1)S(1)}, bf16[128,1024]{1,0:T(8,128)(2,1)S(1)}, u32[]{:S(2)}, u32[]{:S(2)}) %collective-permute-start.2) | collective-permute-done | bytes 262176 | tf_op jit(solution)/shard_map/ppermute | solution.py:24
  32.5 1.6 collective-permute-start.17
  34.1 3.1 %collective-permute-done.12 = bf16[32,2560]{1,0:T(8,128)(2,1)S(1)} collective-permute-done((bf16[32,2560]{1,0:T(8,128)(2,1)S(1)}, bf16[32,2560]{1,0:T(8,128)(2,1)S(1)}, u32[]{:S(2)}, u32[]{:S(2)}) %collective-permute-start.12) | collective-permute-done | bytes 163872 | tf_op jit(solution)/shard_map/ppermute | solution.py:24
  37.2 1.6 collective-permute-start.16
  44.5 7.1 %collective-permute-done.16.refs_10_ = bf16[80,2560]{1,0:T(8,128)(2,1)} collective-permute-done((bf16[80,2560]{1,0:T(8,128)(2,1)S(1)}, bf16[80,2560]{1,0:T(8,128)(2,1)}, u32[]{:S(2)}, u32[]{:S(2)}) %collective-permute-start.16) | collective-permute-done | bytes 409632 | tf_op jit(solution)/shard_map/ppermute | solution.py:169
  52.3 10.6 %attention.1.refs_1_ = bf16[128,2560]{1,0:T(8,128)(2,1)} custom-call(s32[9]{0:T(128)} %stack.55.refs_0_, bf16[128,2560]{1,0:T(8,128)(2,1)} %refs_1_.2, bf16[128,1024]{1,0:T(8,128)(2,1)} %copy-done.1, bf16[128,1024]{1,0:T(8,128)(2,1)} %copy-done.2, bf16[128,1024]{1,0:T(8,128)(2,1)} %copy-done.6, bf16[128,1024]{1,0:T(8,128)(2,1)} %copy-done.3, ...), custom_call_target="tpu_custom_call" | custom-call | tf_op jit(solution)/shard_map/attention/pallas_call | solution.py:88
  66.7 2.2 %collective-permute-done.20.refs_14_ = bf16[80,2560]{1,0:T(8,128)(2,1)} collective-permute-done((bf16[80,2560]{1,0:T(8,128)(2,1)}, bf16[80,2560]{1,0:T(8,128)(2,1)}, u32[]{:S(2)}, u32[]{:S(2)}) %collective-permute-start.20) | collective-permute-done | bytes 409632 | tf_op jit(solution)/shard_map/ppermute | solution.py:169
  70.6 4.9 %collective-permute-done.19.refs_13_ = bf16[80,2560]{1,0:T(8,128)(2,1)S(1)} collective-permute-done((bf16[80,2560]{1,0:T(8,128)(2,1)S(1)}, bf16[80,2560]{1,0:T(8,128)(2,1)S(1)}, u32[]{:S(2)}, u32[]{:S(2)}) %collective-permute-start.19) | collective-permute-done | bytes 409632 | tf_op jit(solution)/shard_map/ppermute | solution.py:24
  75.9 7.9 %collective-permute-done.23.refs_17_ = bf16[80,2560]{1,0:T(8,128)(2,1)S(1)} collective-permute-done((bf16[80,2560]{1,0:T(8,128)(2,1)}, bf16[80,2560]{1,0:T(8,128)(2,1)S(1)}, u32[]{:S(2)}, u32[]{:S(2)}) %collective-permute-start.23) | collective-permute-done | bytes 409632 | tf_op jit(solution)/shard_map/ppermute | solution.py:24
  84.5 7.1 %project_half.1 = (bf16[4,128,384]{2,1,0:T(8,128)(2,1)}, bf16[4,128,384]{2,1,0:T(8,128)(2,1)}) custom-call(s32[3]{0:T(128)} %pad_add_fusion.refs_0_, bf16[128,2560]{1,0:T(8,128)(2,1)} %attention.1.refs_1_, bf16[128,2560]{1,0:T(8,128)(2,1)} %copy-done.13, bf16[80,2560]{1,0:T(8,128)(2,1)} %bitcast.24, bf16[80,2560]{1,0:T(8,128)(2,1)} %copy-done.12, ...), custom_call_target="tpu_custom_call" | custom-call | tf_op jit(solution)/shard_map/project_half/pallas_call | solution.py:224
  94.4 4.1 %merge.1 = (bf16[128,2560]{1,0:T(8,128)(2,1)}, bf16[256,2560]{1,0:T(8,128)(2,1)}) custom-call(s32[3]{0:T(128)} %pad_add_fusion.refs_0_, bf16[4,128,384]{2,1,0:T(8,128)(2,1)} %get-tuple-element.6.refs_1_, bf16[4,128,384]{2,1,0:T(8,128)(2,1)} %copy-done.19, bf16[128,2560]{1,0:T(8,128)(2,1)} %refs_3_.1, f32[1,2560]{1,0:T(1,128)} %reshape.43.refs_4_, ...), custom_call_target="tpu_custom_call" | custom-call | tf_op jit(solution)/shard_map/merge/pallas_call | solution.py:274
  98.6 38.8 %all_to_all.10 = bf16[32,8,2560]{2,1,0:T(8,128)(2,1)} all-to-all(bf16[32,8,2560]{2,1,0:T(8,128)(2,1)} %bitcast.20), channel_id=1, replica_groups=mesh['seq'=32] {'seq'}, dimensions={0} | all-to-all | bytes 2621440 | tf_op jit(solution)/shard_map/all_to_all | solution.py:490
  137.4 21.7 %experts.1 = bf16[256,2560]{1,0:T(8,128)(2,1)} custom-call(bf16[256,2560]{1,0:T(8,128)(2,1)} %bitcast.18, bf16[2560,2,3328]{2,1,0:T(2,128)(2,1)} %refs_1_.3, bf16[3328,2560]{1,0:T(8,128)(2,1)} %refs_2_.1), custom_call_target="tpu_custom_call" | custom-call | tf_op jit(solution)/shard_map/experts/pallas_call | solution.py:371
  159.1 2.7 %all-to-all-start.1 = ((bf16[32,8,2560]{2,1,0:T(8,128)(2,1)}), bf16[32,8,2560]{2,1,0:T(8,128)(2,1)S(1)}, u32[]{:S(2)}, u32[]{:S(2)}) async-start(bf16[32,8,2560]{2,1,0:T(8,128)(2,1)} %bitcast.17), calls=%async_computation.1 | async-start | bytes 2621440 | tf_op jit(solution)/shard_map/all_to_all | solution.py:497
  162.7 30.9 %all-to-all-done.1 = bf16[32,8,2560]{2,1,0:T(8,128)(2,1)S(1)} async-done(((bf16[32,8,2560]{2,1,0:T(8,128)(2,1)}), bf16[32,8,2560]{2,1,0:T(8,128)(2,1)S(1)}, u32[]{:S(2)}, u32[]{:S(2)}) %all-to-all-start.1) | async-done | bytes 1310752 | tf_op jit(solution)/shard_map/all_to_all | solution.py:497
  194.8 2.5 %combine.1 = bf16[128,2560]{1,0:T(8,128)(2,1)} custom-call(bf16[128,256]{1,0:T(8,128)(2,1)} %get-tuple-element.21.high_ref, bf16[128,256]{1,0:T(8,128)(2,1)} %get-tuple-element.20.low_ref, bf16[256,2560]{1,0:T(8,128)(2,1)} %bitcast.19), custom_call_target="tpu_custom_call" | custom-call | tf_op jit(solution)/shard_map/combine/pallas_call | solution.py:418
  (113 shorter events, 23.9 us)
Async XLA Ops:
  0.6 12.7 %collective-permute-start.10 = (bf16[80,2560]{1,0:T(8,128)(2,1)}, bf16[80,2560]{1,0:T(8,128)(2,1)S(1)}, u32[]{:S(2)}, u32[]{:S(2)}) collective-permute-start(bf16[80,2560]{1,0:T(8,128)(2,1)} %bitcast.21), channel_id=1, source_target_pairs={{0,4},{1,5},{2,6},{3,7},{4,0},{5,1},{6,2},{7,3},{8,12},{9,13},{10,... | collective-permute-start | bytes 1228808 | tf_op jit(solution)/shard_map/ppermute | solution.py:24
  5.5 10.2 %collective-permute-start = (bf16[128,1024]{1,0:T(8,128)(2,1)S(1)}, bf16[128,1024]{1,0:T(8,128)(2,1)S(1)}, u32[]{:S(2)}, u32[]{:S(2)}) collective-permute-start(bf16[128,1024]{1,0:T(8,128)(2,1)S(1)} %constant_dynamic-update-slice_fusion.refs_2_.refs_11_), channel_id=1, source_target_pairs={{0,8},{1,9},{2,10},{3,11},{4,12},{5,13},{6,14},{7,15},{8,16},{9,17... | collective-permute-start | bytes 786440 | tf_op jit(solution)/shard_map/ppermute | solution.py:29
  9.0 12.6 %collective-permute-start.9 = (bf16[80,2560]{1,0:T(8,128)(2,1)}, bf16[80,2560]{1,0:T(8,128)(2,1)S(1)}, u32[]{:S(2)}, u32[]{:S(2)}) collective-permute-start(bf16[80,2560]{1,0:T(8,128)(2,1)} %bitcast.22), channel_id=1, source_target_pairs={{0,2},{1,3},{2,0},{3,1},{4,6},{5,7},{6,4},{7,5},{8,10},{9,11},{10,... | collective-permute-start | bytes 1228808 | tf_op jit(solution)/shard_map/ppermute | solution.py:24
  10.6 16.9 %collective-permute-start.13 = (bf16[80,2560]{1,0:T(8,128)(2,1)}, bf16[80,2560]{1,0:T(8,128)(2,1)S(1)}, u32[]{:S(2)}, u32[]{:S(2)}) collective-permute-start(bf16[80,2560]{1,0:T(8,128)(2,1)} %bitcast.23), channel_id=1, source_target_pairs={{0,8},{1,9},{2,10},{3,11},{4,12},{5,13},{6,14},{7,15},{8,16},{9,17... | collective-permute-start | bytes 1228808 | tf_op jit(solution)/shard_map/ppermute | solution.py:169
  13.4 13.5 %collective-permute-start.11 = (bf16[48,2560]{1,0:T(8,128)(2,1)S(1)}, bf16[48,2560]{1,0:T(8,128)(2,1)S(1)}, u32[]{:S(2)}, u32[]{:S(2)}) collective-permute-start(bf16[48,2560]{1,0:T(8,128)(2,1)S(1)} %slice.16), channel_id=1, source_target_pairs={{0,2},{1,3},{2,0},{3,1},{4,6},{5,7},{6,4},{7,5},{8,10},{9,11},{10,... | collective-permute-start | bytes 737288 | tf_op jit(solution)/shard_map/ppermute | solution.py:24
  15.8 16.8 %collective-permute-start.2 = (bf16[128,1024]{1,0:T(8,128)(2,1)S(1)}, bf16[128,1024]{1,0:T(8,128)(2,1)S(1)}, u32[]{:S(2)}, u32[]{:S(2)}) collective-permute-start(bf16[128,1024]{1,0:T(8,128)(2,1)S(1)} %get-tuple-element.18), channel_id=1, source_target_pairs={{0,2},{1,3},{2,0},{3,1},{4,6},{5,7},{6,4},{7,5},{8,10},{9,11},{10,... | collective-permute-start | bytes 786440 | tf_op jit(solution)/shard_map/ppermute | solution.py:24
  17.3 19.9 %collective-permute-start.4 = (bf16[128,1024]{1,0:T(8,128)(2,1)S(1)}, bf16[128,1024]{1,0:T(8,128)(2,1)S(1)}, u32[]{:S(2)}, u32[]{:S(2)}) collective-permute-start(bf16[128,1024]{1,0:T(8,128)(2,1)S(1)} %get-tuple-element.17), channel_id=1, source_target_pairs={{0,4},{1,5},{2,6},{3,7},{4,0},{5,1},{6,2},{7,3},{8,12},{9,13},{10,... | collective-permute-start | bytes 786440 | tf_op jit(solution)/shard_map/ppermute | solution.py:24
  21.7 17.2 %collective-permute-start.6 = (bf16[128,1024]{1,0:T(8,128)(2,1)S(1)}, bf16[128,1024]{1,0:T(8,128)(2,1)S(1)}, u32[]{:S(2)}, u32[]{:S(2)}) collective-permute-start(bf16[128,1024]{1,0:T(8,128)(2,1)S(1)} %get-tuple-element.16), channel_id=1, source_target_pairs={{0,6},{1,7},{2,4},{3,5},{4,2},{5,3},{6,0},{7,1},{8,14},{9,15},{10,... | collective-permute-start | bytes 786440 | tf_op jit(solution)/shard_map/ppermute | solution.py:24
  26.9 10.2 %collective-permute-start.12 = (bf16[32,2560]{1,0:T(8,128)(2,1)S(1)}, bf16[32,2560]{1,0:T(8,128)(2,1)S(1)}, u32[]{:S(2)}, u32[]{:S(2)}) collective-permute-start(bf16[32,2560]{1,0:T(8,128)(2,1)S(1)} %slice.17), channel_id=1, source_target_pairs={{0,4},{1,5},{2,6},{3,7},{4,0},{5,1},{6,2},{7,3},{8,12},{9,13},{10,... | collective-permute-start | bytes 491528 | tf_op jit(solution)/shard_map/ppermute | solution.py:24
  27.5 11.6 %collective-permute-start.1 = (bf16[128,1024]{1,0:T(8,128)(2,1)S(1)}, bf16[128,1024]{1,0:T(8,128)(2,1)S(1)}, u32[]{:S(2)}, u32[]{:S(2)}) collective-permute-start(bf16[128,1024]{1,0:T(8,128)(2,1)S(1)} %get-tuple-element.19), channel_id=1, source_target_pairs={{0,1},{1,0},{2,3},{3,2},{4,5},{5,4},{6,7},{7,6},{8,9},{9,8},{10,11... | collective-permute-start | bytes 786440 | tf_op jit(solution)/shard_map/ppermute | solution.py:24
  32.5 10.1 %collective-permute-start.17 = (bf16[80,2560]{1,0:T(8,128)(2,1)S(1)}, bf16[80,2560]{1,0:T(8,128)(2,1)S(1)}, u32[]{:S(2)}, u32[]{:S(2)}) collective-permute-start(bf16[80,2560]{1,0:T(8,128)(2,1)S(1)} %collective-permute-done.13.refs_7_), channel_id=1, source_target_pairs={{0,8},{1,9},{2,10},{3,11},{4,12},{5,13},{6,14},{7,15},{8,16},{9,17... | collective-permute-start | bytes 1228808 | tf_op jit(solution)/shard_map/ppermute | solution.py:169
  37.2 14.3 %collective-permute-start.16 = (bf16[80,2560]{1,0:T(8,128)(2,1)S(1)}, bf16[80,2560]{1,0:T(8,128)(2,1)}, u32[]{:S(2)}, u32[]{:S(2)}) collective-permute-start(bf16[80,2560]{1,0:T(8,128)(2,1)S(1)} %constant_dynamic-update-slice_fusion.2.refs_6_), channel_id=1, source_target_pairs={{0,8},{1,9},{2,10},{3,11},{4,12},{5,13},{6,14},{7,15},{8,16},{9,17... | collective-permute-start | bytes 1228808 | tf_op jit(solution)/shard_map/ppermute | solution.py:169
  39.1 4.4 %collective-permute-start.7 = (bf16[128,1024]{1,0:T(8,128)(2,1)S(1)}, bf16[128,1024]{1,0:T(8,128)(2,1)S(1)}, u32[]{:S(2)}, u32[]{:S(2)}) collective-permute-start(bf16[128,1024]{1,0:T(8,128)(2,1)S(1)} %collective-permute-done.6.refs_9_.refs_18_), channel_id=1, source_target_pairs={{0,1},{1,0},{2,3},{3,2},{4,5},{5,4},{6,7},{7,6},{8,9},{9,8},{10,11... | collective-permute-start | bytes 786440 | tf_op jit(solution)/shard_map/ppermute | solution.py:24
  39.4 23.5 %collective-permute-start.14 = (bf16[80,2560]{1,0:T(8,128)(2,1)S(1)}, bf16[80,2560]{1,0:T(8,128)(2,1)}, u32[]{:S(2)}, u32[]{:S(2)}) collective-permute-start(bf16[80,2560]{1,0:T(8,128)(2,1)S(1)} %collective-permute-done.13.refs_7_), channel_id=1, source_target_pairs={{0,2},{1,3},{2,0},{3,1},{4,6},{5,7},{6,4},{7,5},{8,10},{9,11},{10,... | collective-permute-start | bytes 1228808 | tf_op jit(solution)/shard_map/ppermute | solution.py:24
  40.9 22.2 %collective-permute-start.15 = (bf16[80,2560]{1,0:T(8,128)(2,1)S(1)}, bf16[80,2560]{1,0:T(8,128)(2,1)}, u32[]{:S(2)}, u32[]{:S(2)}) collective-permute-start(bf16[80,2560]{1,0:T(8,128)(2,1)S(1)} %collective-permute-done.13.refs_7_), channel_id=1, source_target_pairs={{0,4},{1,5},{2,6},{3,7},{4,0},{5,1},{6,2},{7,3},{8,12},{9,13},{10,... | collective-permute-start | bytes 1228808 | tf_op jit(solution)/shard_map/ppermute | solution.py:24
  42.7 21.4 %collective-permute-start.21 = (bf16[80,2560]{1,0:T(8,128)(2,1)S(1)}, bf16[80,2560]{1,0:T(8,128)(2,1)}, u32[]{:S(2)}, u32[]{:S(2)}) collective-permute-start(bf16[80,2560]{1,0:T(8,128)(2,1)S(1)} %collective-permute-done.17.refs_11_), channel_id=1, source_target_pairs={{0,8},{1,9},{2,10},{3,11},{4,12},{5,13},{6,14},{7,15},{8,16},{9,17... | collective-permute-start | bytes 1228808 | tf_op jit(solution)/shard_map/ppermute | solution.py:169
  43.5 22.1 %collective-permute-start.18 = (bf16[80,2560]{1,0:T(8,128)(2,1)S(1)}, bf16[80,2560]{1,0:T(8,128)(2,1)}, u32[]{:S(2)}, u32[]{:S(2)}) collective-permute-start(bf16[80,2560]{1,0:T(8,128)(2,1)S(1)} %collective-permute-done.17.refs_11_), channel_id=1, source_target_pairs={{0,2},{1,3},{2,0},{3,1},{4,6},{5,7},{6,4},{7,5},{8,10},{9,11},{10,... | collective-permute-start | bytes 1228808 | tf_op jit(solution)/shard_map/ppermute | solution.py:24
  51.6 17.3 %collective-permute-start.20 = (bf16[80,2560]{1,0:T(8,128)(2,1)}, bf16[80,2560]{1,0:T(8,128)(2,1)}, u32[]{:S(2)}, u32[]{:S(2)}) collective-permute-start(bf16[80,2560]{1,0:T(8,128)(2,1)} %collective-permute-done.16.refs_10_), channel_id=1, source_target_pairs={{0,8},{1,9},{2,10},{3,11},{4,12},{5,13},{6,14},{7,15},{8,16},{9,17... | collective-permute-start | bytes 1228808 | tf_op jit(solution)/shard_map/ppermute | solution.py:169
  62.9 12.6 %collective-permute-start.8 = (bf16[128,2560]{1,0:T(8,128)(2,1)}, bf16[128,2560]{1,0:T(8,128)(2,1)S(1)}, u32[]{:S(2)}, u32[]{:S(2)}) collective-permute-start(bf16[128,2560]{1,0:T(8,128)(2,1)} %attention.1.refs_1_), channel_id=1, source_target_pairs={{0,1},{1,0},{2,3},{3,2},{4,5},{5,4},{6,7},{7,6},{8,9},{9,8},{10,11... | collective-permute-start | bytes 1966088 | tf_op jit(solution)/shard_map/ppermute | solution.py:24
  63.1 12.4 %collective-permute-start.19 = (bf16[80,2560]{1,0:T(8,128)(2,1)S(1)}, bf16[80,2560]{1,0:T(8,128)(2,1)S(1)}, u32[]{:S(2)}, u32[]{:S(2)}) collective-permute-start(bf16[80,2560]{1,0:T(8,128)(2,1)S(1)} %collective-permute-done.17.refs_11_), channel_id=1, source_target_pairs={{0,4},{1,5},{2,6},{3,7},{4,0},{5,1},{6,2},{7,3},{8,12},{9,13},{10,... | collective-permute-start | bytes 1228808 | tf_op jit(solution)/shard_map/ppermute | solution.py:24
  64.1 11.8 %collective-permute-start.22 = (bf16[80,2560]{1,0:T(8,128)(2,1)}, bf16[80,2560]{1,0:T(8,128)(2,1)S(1)}, u32[]{:S(2)}, u32[]{:S(2)}) collective-permute-start(bf16[80,2560]{1,0:T(8,128)(2,1)} %collective-permute-done.21.refs_15_), channel_id=1, source_target_pairs={{0,2},{1,3},{2,0},{3,1},{4,6},{5,7},{6,4},{7,5},{8,10},{9,11},{10,... | collective-permute-start | bytes 1228808 | tf_op jit(solution)/shard_map/ppermute | solution.py:24
  65.6 18.2 %collective-permute-start.23 = (bf16[80,2560]{1,0:T(8,128)(2,1)}, bf16[80,2560]{1,0:T(8,128)(2,1)S(1)}, u32[]{:S(2)}, u32[]{:S(2)}) collective-permute-start(bf16[80,2560]{1,0:T(8,128)(2,1)} %collective-permute-done.21.refs_15_), channel_id=1, source_target_pairs={{0,4},{1,5},{2,6},{3,7},{4,0},{5,1},{6,2},{7,3},{8,12},{9,13},{10,... | collective-permute-start | bytes 1228808 | tf_op jit(solution)/shard_map/ppermute | solution.py:24
  68.9 14.9 %collective-permute-start.24 = (bf16[80,2560]{1,0:T(8,128)(2,1)}, bf16[80,2560]{1,0:T(8,128)(2,1)}, u32[]{:S(2)}, u32[]{:S(2)}) collective-permute-start(bf16[80,2560]{1,0:T(8,128)(2,1)} %collective-permute-done.20.refs_14_), channel_id=1, source_target_pairs={{0,8},{1,9},{2,10},{3,11},{4,12},{5,13},{6,14},{7,15},{8,16},{9,17... | collective-permute-start | bytes 1228808 | tf_op jit(solution)/shard_map/ppermute | solution.py:169
  159.1 34.6 %all-to-all-start.1 = ((bf16[32,8,2560]{2,1,0:T(8,128)(2,1)}), bf16[32,8,2560]{2,1,0:T(8,128)(2,1)S(1)}, u32[]{:S(2)}, u32[]{:S(2)}) async-start(bf16[32,8,2560]{2,1,0:T(8,128)(2,1)} %bitcast.17), calls=%async_computation.1 | async-start | bytes 2621440 | tf_op jit(solution)/shard_map/all_to_all | solution.py:497
  (28 other events, 438.4 us)
